TPU v7x, 128 devices: a whole 4x4x4 slice. The times are simulated.
128 devices in a mesh: fsdp: 8 (over z_hi, y), tp: 16 (over z_lo, x, core).
Axes of the slice: x: 4, y: 4, z: 4 (z_hi: 2, z_lo: 2; z = z_hi * 2 + z_lo), core: 2. Of those that a mesh axis runs over, the one named last changes fastest.
Arguments:
- tokens: bfloat16 [2048, 8192], P('fsdp', 'tp'), may hold values from -6 to 6
- out_grad: bfloat16 [2048, 8192], P('fsdp', 'tp'), may hold values from -6 to 6
- gate_weight: bfloat16 [8192, 2048], P('fsdp', 'tp'), may hold values from -0.0625 to 0.0625
- up_weight: bfloat16 [8192, 2048], P('fsdp', 'tp'), may hold values from -0.0625 to 0.0625
- down_weight: bfloat16 [2048, 8192], P('tp', 'fsdp'), may hold values from -0.125 to 0.125
Outputs:
- input_grad: bfloat16 [2048, 8192], P('fsdp', 'tp')
- gate_grad: float32 [8192, 2048], P('fsdp', 'tp')
- up_grad: float32 [8192, 2048], P('fsdp', 'tp')
- down_grad: float32 [2048, 8192], P('tp', 'fsdp')
All inputs are finite; a program needn't handle non-finite values.
Results may differ from a plain program's by a relative error of at most 0.0023.
Values may be sent and summed in bfloat16 or wider, within the bound.
No kernel may reach another device: no remote copies, remote signals or barrier semaphores. Data moves between devices by JAX's collectives and lax.ppermute only.
A program may use at most 128 MiB of HBM per device.

v0:
```python
import functools
import math

import jax
import jax.numpy as jnp
from jax import lax
from jax.experimental import pallas as pl
from jax.experimental.pallas import tpu as pltpu
from jax.sharding import Mesh
from jax.sharding import PartitionSpec as P

AXES = ("zh", "y", "zl", "x", "c")
SIZES = (2, 4, 2, 4, 2)
BF16 = jnp.bfloat16
F32 = jnp.float32
STEPS = (1, 3, 2)
F16 = jnp.float16
TOP = 14.0
NOTE = 16


def number(place):
    at = 0
    for size, coordinate in zip(SIZES, place):
        at = at * size + coordinate
    return at


def places():
    found = [()]
    for size in SIZES:
        found = [(*place, k) for place in found for k in range(size)]
    return found


def moved(value, target, back=False):
    pairs = [(number(p), number(target(*p))) for p in places()]
    if back:
        pairs = [(b, a) for a, b in pairs]
    return lax.ppermute(value, AXES, pairs)


def turned(value, axis, step):
    return lax.ppermute(value, axis, [(i, (i + step) % 4) for i in range(4)])


def other_core(value):
    return lax.ppermute(value, "c", [(0, 1), (1, 0)])


def stay(zh, y, zl, x, c):
    return (zh, x, zl, (x - y) % 4, c)


def cross(zh, y, zl, x, c):
    return (zh, x, 1 - zl, (x - y) % 4, c)


def along_z(value, mask):
    return moved(value, lambda zh, y, zl, x, c: (zh ^ (mask >> 1), y, zl ^ (mask & 1), x, c))


def call(body, scalars, arrays, outs, flops):
    smem = pl.BlockSpec(memory_space=pltpu.SMEM)
    vmem = pl.BlockSpec(memory_space=pltpu.VMEM)
    return pl.pallas_call(
        body,
        in_specs=[smem] * len(scalars) + [vmem] * len(arrays),
        out_specs=[vmem] * len(outs),
        out_shape=[jax.ShapeDtypeStruct(s, t) for s, t in outs],
        compiler_params=pltpu.CompilerParams(vmem_limit_bytes=8 * 1024 * 1024),
        cost_estimate=pl.CostEstimate(flops=flops, bytes_accessed=1 << 20, transcendentals=0),
    )(*scalars, *arrays)


def dot(a, b, da, db):
    return lax.dot_general(a, b, (((da,), (db,)), ((), ())), preferred_element_type=F32)


def pack_kernel(flag_ref, p_ref, q_ref, out_ref):
    wide = p_ref.shape[1]

    @pl.when(flag_ref[0] == 0)
    def _():
        out_ref[:, :wide] = p_ref[...]
        out_ref[:, wide:] = q_ref[...]

    @pl.when(flag_ref[0] != 0)
    def _():
        out_ref[:, :wide] = q_ref[...]
        out_ref[:, wide:] = p_ref[...]


def join_kernel(a_ref, b_ref, out_ref):
    wide = a_ref.shape[1]
    out_ref[:, :wide] = a_ref[...]
    out_ref[:, wide:] = b_ref[...]


def stacked(refs, at):
    return jnp.concatenate([r[:, at] for r in refs], axis=0)


def put_parts(outs, pieces, half):
    largest = None
    for _, value in pieces:
        size = jnp.max(jnp.abs(value), axis=(0, 1), keepdims=True)
        largest = size if largest is None else jnp.maximum(largest, size)
    exponent = jnp.clip(jnp.floor(jnp.log2(largest)), -100.0, 100.0)
    scale = jnp.exp2(TOP - exponent)
    for at, value in pieces:
        outs[0][:, at] = value[:half]
        for k in (1, 2, 3):
            outs[k][:half, at] = value[k * half : (k + 1) * half] * scale
    for k in (1, 2, 3):
        outs[k][half:, :] = jnp.broadcast_to(exponent, (NOTE, outs[k].shape[1]))


def forward_kernel(core_ref, *refs, transposed, kinds):
    own, other, weights, outs = refs[:4], refs[4:8], refs[8:12], refs[12:16]
    core = core_ref[0]
    half = own[0].shape[0]
    deep = own[0].shape[1] // 2
    totals = [None, None]
    for side, rows in ((core, own), (1 - core, other)):
        at = pl.ds(pl.multiple_of(side * deep, deep), deep)
        for a in (0, 1):
            block = stacked(rows, slice(a * deep, (a + 1) * deep))
            for b in (0, 1):
                if transposed:
                    term = dot(block, weights[2 * a + b][:, at], 1, 1)
                else:
                    term = dot(block, weights[2 * a + b][at, :], 1, 0)
                totals[b] = term if totals[b] is None else totals[b] + term
    units = totals[0].shape[1] // kinds
    pieces = []
    for b in (0, 1):
        for kind in range(kinds):
            place = (2 * kind + b) * units
            pieces.append((slice(place, place + units), totals[b][:, kind * units : (kind + 1) * units]))
    put_parts(outs, pieces, half)


def activation_kernel(sum_ref, hidden_ref, slope_ref, activated_ref):
    width = hidden_ref.shape[1]
    gate, up = sum_ref[:, :width], sum_ref[:, width:]
    squashed = jax.nn.sigmoid(gate)
    activated = gate * squashed
    hidden_ref[...] = (activated * up).astype(BF16)
    slope_ref[...] = up * (squashed * (1.0 + gate * (1.0 - squashed)))
    activated_ref[...] = activated


def delta_kernel(grad_ref, slope_ref, activated_ref, out_ref):
    width = grad_ref.shape[1]
    out_ref[:, :width] = (grad_ref[...] * slope_ref[...]).astype(BF16)
    out_ref[:, width:] = (grad_ref[...] * activated_ref[...]).astype(BF16)


def delta_columns(refs, b):
    units = refs[0].shape[1] // 4
    return jnp.concatenate(
        [stacked(refs, slice((2 * kind + b) * units, (2 * kind + b + 1) * units)) for kind in (0, 1)], axis=1
    )


def down_grad_kernel(core_ref, *refs, factor):
    hidden, own, other, outs = refs[:4], refs[4:8], refs[8:12], refs[12:16]
    core = core_ref[0]
    deep = own[0].shape[1] // 2
    units = hidden[0].shape[1] // 2
    left = stacked(hidden, slice(None))
    for side, rows in ((core, own), (1 - core, other)):
        at = pl.ds(pl.multiple_of(side * deep, deep), deep)
        for a in (0, 1):
            total = dot(left, stacked(rows, slice(a * deep, (a + 1) * deep)), 0, 0)
            for b in (0, 1):
                out = outs[2 * a + b]
                out[:, at] = (total[b * units : (b + 1) * units] * factor).astype(out.dtype)


def gate_up_grad_kernel(core_ref, *refs, factor):
    deltas, own, other, outs = refs[:4], refs[4:8], refs[8:12], refs[12:16]
    core = core_ref[0]
    deep = own[0].shape[1] // 2
    right = [delta_columns(deltas, b) for b in (0, 1)]
    for side, rows in ((core, own), (1 - core, other)):
        at = pl.ds(pl.multiple_of(side * deep, deep), deep)
        for a in (0, 1):
            left = stacked(rows, slice(a * deep, (a + 1) * deep))
            for b in (0, 1):
                out = outs[2 * a + b]
                out[at, :] = (dot(left, right[b], 0, 0) * factor).astype(out.dtype)


def input_grad_kernel(core_ref, *refs):
    deltas, weights, outs = (refs[:4], refs[4:8]), (refs[8:12], refs[12:16]), refs[16:20]
    half = deltas[0][0].shape[0]
    deep = weights[0][0].shape[0] // 2
    at = pl.ds(pl.multiple_of(core_ref[0] * deep, deep), deep)
    left = [[delta_columns(deltas[side], b) for b in (0, 1)] for side in (0, 1)]
    pieces = []
    for a in (0, 1):
        total = None
        for side in (0, 1):
            for b in (0, 1):
                term = dot(left[side][b], weights[side][2 * a + b][at, :], 1, 1)
                total = term if total is None else total + term
        pieces.append((slice(a * deep, (a + 1) * deep), total))
    put_parts(outs, pieces, half)


def step(tokens, out_grad, gate_weight, up_weight, down_weight):
    factor = 1.0 / math.sqrt(tokens.shape[0] * 8)
    zh, zl, c = lax.axis_index("zh"), lax.axis_index("zl"), lax.axis_index("c")
    half = tokens.shape[0] // 2
    deep = gate_weight.shape[0] // 2
    units = gate_weight.shape[1]
    width = 2 * units
    uneven = (zh ^ zl).reshape(1)
    core = c.reshape(1)
    wide = 2 * deep

    def to_block(value):
        mine = lax.dynamic_slice_in_dim(value, zl * half, half, 0)
        theirs = lax.dynamic_slice_in_dim(value, (1 - zl) * half, half, 0)
        p, q = moved(mine, stay), moved(theirs, cross)
        return call(pack_kernel, [uneven], [p, q], [((half, wide), tokens.dtype)], 1000)[0]

    def over_x(block):
        rows = {0: block}
        for k in STEPS:
            rows[k] = turned(block, "x", k)
        other = {k: other_core(rows[k]) for k in (0, *STEPS)}
        return [rows[k] for k in range(4)], [other[k] for k in range(4)]

    def pieces(value):
        found = {0: value}
        for m in STEPS:
            found[m] = along_z(value, m)
        return [found[m] for m in range(4)]

    x_own, x_other = over_x(to_block(tokens))
    g_own, g_other = over_x(to_block(out_grad))
    joined = call(join_kernel, [], [gate_weight, up_weight], [((wide, width), BF16)], 1000)[0]
    gu = pieces(joined)
    down = pieces(down_weight)

    gu_other = [other_core(gu[m]) for m in range(4)]

    def parts_of(columns):
        return [((half, columns), F32)] + [((half + NOTE, columns), F32)] * 3

    gu_flops = 2 * 4 * half * 4 * deep * 2 * width
    gu_parts = call(
        functools.partial(forward_kernel, transposed=False, kinds=2), [core],
        [*x_own, *x_other, *gu], parts_of(2 * width), gu_flops,
    )
    down_parts = call(
        functools.partial(forward_kernel, transposed=True, kinds=1), [core],
        [*g_own, *g_other, *down], parts_of(width), gu_flops // 2,
    )

    def summed(parts, axis):
        total = parts[0]
        sent = [p.astype(F16) for p in parts]
        for k in STEPS:
            got = turned(sent[k], axis, k).astype(F32)
            total = total + got[:half] * jnp.exp2(got[half : half + 1] - TOP)
        return total

    gate_up = summed(gu_parts, "y")
    hidden_grad = summed(down_parts, "y")
    hidden, slope, activated = call(
        activation_kernel, [], [gate_up],
        [((half, width), BF16), ((half, width), F32), ((half, width), F32)], 1000,
    )
    deltas = call(delta_kernel, [], [hidden_grad, slope, activated], [((half, 2 * width), BF16)], 1000)[0]

    def over_y(block):
        rows = {0: block}
        for k in STEPS:
            rows[k] = turned(block, "y", k)
        return [rows[k] for k in range(4)]

    hidden_rows = over_y(hidden)
    delta_rows = over_y(deltas)
    delta_other = [other_core(delta_rows[k]) for k in range(4)]

    def matching(rows):
        return [rows[0], rows[3], rows[2], rows[1]]

    down_out = call(
        functools.partial(down_grad_kernel, factor=factor), [core],
        [*matching(hidden_rows), *g_own, *g_other],
        [((units, wide), F32)] + [((units, wide), BF16)] * 3, gu_flops // 2,
    )
    ig_parts = call(
        input_grad_kernel, [core], [*delta_rows, *delta_other, *gu, *gu_other],
        parts_of(wide), gu_flops,
    )
    gu_out = call(
        functools.partial(gate_up_grad_kernel, factor=factor), [core],
        [*matching(delta_rows), *x_own, *x_other],
        [((wide, width), F32)] + [((wide, width), BF16)] * 3, gu_flops,
    )

    def from_z(outs):
        return [outs[0]] + [along_z(outs[m], m) for m in STEPS]

    def total_of(terms, at):
        total = terms[0][:, at]
        for term in terms[1:]:
            total = total + term[:, at].astype(F32)
        return total

    down_grad = total_of(from_z(down_out), slice(None))
    gu_terms = from_z(gu_out)
    gate_grad, up_grad = total_of(gu_terms, slice(0, units)), total_of(gu_terms, slice(units, width))

    total = summed(ig_parts, "x").astype(BF16)
    kept = jnp.where(zh == zl, total[:, :deep], total[:, deep:])
    sent = jnp.where(zh == zl, total[:, deep:], total[:, :deep])
    kept, sent = moved(kept, stay, back=True), moved(sent, cross, back=True)
    input_grad = jnp.concatenate([jnp.where(zl == 0, kept, sent), jnp.where(zl == 0, sent, kept)], axis=0)
    return (input_grad, gate_grad, up_grad, down_grad)


def solution(mesh):
    finer = Mesh(mesh.devices.reshape(SIZES), AXES)
    rows, columns = ("zh", "y"), ("zl", "x", "c")
    return jax.shard_map(
        step,
        mesh=finer,
        in_specs=(P(rows, columns),) * 4 + (P(columns, rows),),
        out_specs=(P(rows, columns),) * 3 + (P(columns, rows),),
        check_vma=False,
    )
```

profile of v0, /device:TPU:0, one launch (start us, length us, event | category | flops | bytes accessed | tf_op | source)
XLA Modules:
  0.0 184.4 jit_solution(1015334174065502611)
XLA Ops:
  0.7 1.0 constant_dynamic-slice_fusion
  2.4 2.1 %collective-permute-start.16 = (bf16[128,512]{1,0:T(8,128)(2,1)S(1)}, bf16[128,512]{1,0:T(8,128)(2,1)S(1)}, u32[]{:S(2)}, u32[]{:S(2)}) collective-permute-start(bf16[128,512]{1,0:T(8,128)(2,1)S(1)} %get-tuple-element.56), channel_id=1, source_target_pairs={{0,8},{1,9},{2,26},{3,27},{4,44},{5,45},{6,62},{7,63},{8,0},{9,1},... | collective-permute-start | bytes 393224 | tf_op jit(solution)/shard_map/ppermute | solution.py:40
  4.5 3.6 %collective-permute-start.10 = (bf16[128,1024]{1,0:T(8,128)(2,1)S(1)}, bf16[128,1024]{1,0:T(8,128)(2,1)S(1)}, u32[]{:S(2)}, u32[]{:S(2)}) collective-permute-start(bf16[128,1024]{1,0:T(8,128)(2,1)S(1)} %copy-done.27), channel_id=1, source_target_pairs={{0,64},{1,65},{2,66},{3,67},{4,68},{5,69},{6,70},{7,71},{8,72},{9,... | collective-permute-start | bytes 786440 | tf_op jit(solution)/shard_map/ppermute | solution.py:40
  8.8 2.1 %collective-permute-start.1 = (bf16[128,512]{1,0:T(8,128)(2,1)S(1)}, bf16[128,512]{1,0:T(8,128)(2,1)S(1)}, u32[]{:S(2)}, u32[]{:S(2)}) collective-permute-start(bf16[128,512]{1,0:T(8,128)(2,1)S(1)} %get-tuple-element.58), channel_id=1, source_target_pairs={{0,8},{1,9},{2,26},{3,27},{4,44},{5,45},{6,62},{7,63},{8,0},{9,1},... | collective-permute-start | bytes 393224 | tf_op jit(solution)/shard_map/ppermute | solution.py:40
  10.9 10.7 %collective-permute-start.17 = (bf16[128,1024]{1,0:T(8,128)(2,1)S(1)}, bf16[128,1024]{1,0:T(8,128)(2,1)}, u32[]{:S(2)}, u32[]{:S(2)}) collective-permute-start(bf16[128,1024]{1,0:T(8,128)(2,1)S(1)} %shard_map.86.refs_0_.refs_4_), channel_id=1, source_target_pairs={{0,2},{2,4},{4,6},{6,0},{1,3},{3,5},{5,7},{7,1},{8,10},{10,12},{12... | collective-permute-start | bytes 786440 | tf_op jit(solution)/shard_map/ppermute | solution.py:44
  22.1 10.0 %collective-permute-start.18 = (bf16[128,1024]{1,0:T(8,128)(2,1)S(1)}, bf16[128,1024]{1,0:T(8,128)(2,1)}, u32[]{:S(2)}, u32[]{:S(2)}) collective-permute-start(bf16[128,1024]{1,0:T(8,128)(2,1)S(1)} %shard_map.86.refs_0_.refs_4_), channel_id=1, source_target_pairs={{0,4},{2,6},{4,0},{6,2},{1,5},{3,7},{5,1},{7,3},{8,12},{10,14},{12... | collective-permute-start | bytes 786440 | tf_op jit(solution)/shard_map/ppermute | solution.py:44
  33.7 1.5 collective-permute-start.24
  35.2 2.1 %collective-permute-start.2 = (bf16[128,1024]{1,0:T(8,128)(2,1)S(1)}, bf16[128,1024]{1,0:T(8,128)(2,1)S(1)}, u32[]{:S(2)}, u32[]{:S(2)}) collective-permute-start(bf16[128,1024]{1,0:T(8,128)(2,1)S(1)} %shard_map.84.refs_0_.refs_4_), channel_id=1, source_target_pairs={{0,2},{2,4},{4,6},{6,0},{1,3},{3,5},{5,7},{7,1},{8,10},{10,12},{12... | collective-permute-start | bytes 786440 | tf_op jit(solution)/shard_map/ppermute | solution.py:44
  37.3 2.8 %collective-permute-start.3 = (bf16[128,1024]{1,0:T(8,128)(2,1)S(1)}, bf16[128,1024]{1,0:T(8,128)(2,1)S(1)}, u32[]{:S(2)}, u32[]{:S(2)}) collective-permute-start(bf16[128,1024]{1,0:T(8,128)(2,1)S(1)} %shard_map.84.refs_0_.refs_4_), channel_id=1, source_target_pairs={{0,4},{2,6},{4,0},{6,2},{1,5},{3,7},{5,1},{7,3},{8,12},{10,14},{12... | collective-permute-start | bytes 786440 | tf_op jit(solution)/shard_map/ppermute | solution.py:44
  40.1 1.0 collective-permute-start.4
  41.8 8.7 %collective-permute-done.2.refs_1_.refs_5_ = bf16[128,1024]{1,0:T(8,128)(2,1)S(1)} collective-permute-done((bf16[128,1024]{1,0:T(8,128)(2,1)S(1)}, bf16[128,1024]{1,0:T(8,128)(2,1)S(1)}, u32[]{:S(2)}, u32[]{:S(2)}) %collective-permute-start.2) | collective-permute-done | bytes 262176 | tf_op jit(solution)/shard_map/ppermute | solution.py:44
  50.5 3.5 %collective-permute-start.25 = (bf16[1024,256]{1,0:T(8,128)(2,1)S(1)}, bf16[1024,256]{1,0:T(8,128)(2,1)S(1)}, u32[]{:S(2)}, u32[]{:S(2)}) collective-permute-start(bf16[1024,256]{1,0:T(8,128)(2,1)S(1)} %shard_map.87.refs_8_), channel_id=1, source_target_pairs={{0,64},{1,65},{2,66},{3,67},{4,68},{5,69},{6,70},{7,71},{8,72},{9,... | collective-permute-start | bytes 1572872 | tf_op jit(solution)/shard_map/ppermute | solution.py:40
  57.6 0.7 copy-done.9
  58.5 0.9 copy-done.1
  59.4 0.9 copy-done.4
  60.4 0.9 copy-done.7
  61.3 0.9 copy-done.10
  62.3 0.9 copy-done.28
  63.2 0.9 copy-done.30
  64.2 0.9 copy-done.32
  65.1 0.9 copy-done.34
  66.1 1.4 shard_map.85
  67.9 9.1 %collective-permute-done.26.refs_11_ = bf16[1024,256]{1,0:T(8,128)(2,1)S(1)} collective-permute-done((bf16[1024,256]{1,0:T(8,128)(2,1)S(1)}, bf16[1024,256]{1,0:T(8,128)(2,1)S(1)}, u32[]{:S(2)}, u32[]{:S(2)}) %collective-permute-start.26) | collective-permute-done | bytes 524320 | tf_op jit(solution)/shard_map/ppermute | solution.py:40
  77.7 2.8 %shard_map.88 = (f32[128,512]{1,0:T(8,128)S(1)}, f32[144,512]{1,0:T(8,128)S(1)}, f32[144,512]{1,0:T(8,128)S(1)}, f32[144,512]{1,0:T(8,128)S(1)}) custom-call(s32[1]{0:T(128)} %bitcast.core_ref, bf16[128,1024]{1,0:T(8,128)(2,1)S(1)} %shard_map.86.refs_0_.refs_4_, bf16[128,1024]{1,0:T(8,128)(2,1)} %collective-permute-done.17.refs_1_.refs_5_, ...), custom_call_target="tpu_custom_call" | custom-call | flops 1073741824 | bytes 1048576 | tf_op jit(solution)/shard_map/pallas_call | solution.py:66
  80.6 2.8 %collective-permute-done.12 = f16[144,256]{1,0:T(8,128)(2,1)S(1)} collective-permute-done((f16[144,256]{1,0:T(8,128)(2,1)S(1)}, f16[144,256]{1,0:T(8,128)(2,1)S(1)}, u32[]{:S(2)}, u32[]{:S(2)}) %collective-permute-start.12) | collective-permute-done | bytes 73760 | tf_op jit(solution)/shard_map/ppermute | solution.py:44
  84.0 3.9 %collective-permute-done.13 = f16[144,256]{1,0:T(8,128)(2,1)S(1)} collective-permute-done((f16[144,256]{1,0:T(8,128)(2,1)S(1)}, f16[144,256]{1,0:T(8,128)(2,1)S(1)}, u32[]{:S(2)}, u32[]{:S(2)}) %collective-permute-start.13) | collective-permute-done | bytes 73760 | tf_op jit(solution)/shard_map/ppermute | solution.py:44
  87.8 6.3 %collective-permute-done.27 = f16[144,512]{1,0:T(8,128)(2,1)S(1)} collective-permute-done((f16[144,512]{1,0:T(8,128)(2,1)S(1)}, f16[144,512]{1,0:T(8,128)(2,1)S(1)}, u32[]{:S(2)}, u32[]{:S(2)}) %collective-permute-start.27) | collective-permute-done | bytes 147488 | tf_op jit(solution)/shard_map/ppermute | solution.py:44
  94.7 4.8 %collective-permute-done.28 = f16[144,512]{1,0:T(8,128)(2,1)S(1)} collective-permute-done((f16[144,512]{1,0:T(8,128)(2,1)S(1)}, f16[144,512]{1,0:T(8,128)(2,1)S(1)}, u32[]{:S(2)}, u32[]{:S(2)}) %collective-permute-start.28) | collective-permute-done | bytes 147488 | tf_op jit(solution)/shard_map/ppermute | solution.py:44
  99.6 7.4 %collective-permute-done.29 = f16[144,512]{1,0:T(8,128)(2,1)S(1)} collective-permute-done((f16[144,512]{1,0:T(8,128)(2,1)S(1)}, f16[144,512]{1,0:T(8,128)(2,1)S(1)}, u32[]{:S(2)}, u32[]{:S(2)}) %collective-permute-start.29) | collective-permute-done | bytes 147488 | tf_op jit(solution)/shard_map/ppermute | solution.py:44
  107.1 6.2 %collective-permute-done.14 = f16[144,256]{1,0:T(8,128)(2,1)S(1)} collective-permute-done((f16[144,256]{1,0:T(8,128)(2,1)S(1)}, f16[144,256]{1,0:T(8,128)(2,1)S(1)}, u32[]{:S(2)}, u32[]{:S(2)}) %collective-permute-start.14) | collective-permute-done | bytes 73760 | tf_op jit(solution)/shard_map/ppermute | solution.py:44
  113.4 1.2 collective-permute-start.49
  114.7 3.0 %collective-permute-done.49.refs_1_ = bf16[128,256]{1,0:T(8,128)(2,1)S(1)} collective-permute-done((bf16[128,256]{1,0:T(8,128)(2,1)S(1)}, bf16[128,256]{1,0:T(8,128)(2,1)S(1)}, u32[]{:S(2)}, u32[]{:S(2)}) %collective-permute-start.49) | collective-permute-done | bytes 65568 | tf_op jit(solution)/shard_map/ppermute | solution.py:44
  117.8 2.9 %collective-permute-done.50.refs_2_ = bf16[128,256]{1,0:T(8,128)(2,1)S(1)} collective-permute-done((bf16[128,256]{1,0:T(8,128)(2,1)S(1)}, bf16[128,256]{1,0:T(8,128)(2,1)S(1)}, u32[]{:S(2)}, u32[]{:S(2)}) %collective-permute-start.50) | collective-permute-done | bytes 65568 | tf_op jit(solution)/shard_map/ppermute | solution.py:44
  120.7 1.3 collective-permute-start.30
  122.0 1.1 collective-permute-done.51.refs_3_
  123.4 3.5 %collective-permute-done.30.refs_1_.refs_3_ = bf16[128,512]{1,0:T(8,128)(2,1)S(1)} collective-permute-done((bf16[128,512]{1,0:T(8,128)(2,1)S(1)}, bf16[128,512]{1,0:T(8,128)(2,1)S(1)}, u32[]{:S(2)}, u32[]{:S(2)}) %collective-permute-start.30) | collective-permute-done | bytes 131104 | tf_op jit(solution)/shard_map/ppermute | solution.py:44
  126.9 2.9 %collective-permute-done.31.refs_2_ = bf16[128,512]{1,0:T(8,128)(2,1)} collective-permute-done((bf16[128,512]{1,0:T(8,128)(2,1)S(1)}, bf16[128,512]{1,0:T(8,128)(2,1)}, u32[]{:S(2)}, u32[]{:S(2)}) %collective-permute-start.31) | collective-permute-done | bytes 131104 | tf_op jit(solution)/shard_map/ppermute | solution.py:44
  129.7 2.2 %collective-permute-done.32.refs_3_.refs_1_ = bf16[128,512]{1,0:T(8,128)(2,1)} collective-permute-done((bf16[128,512]{1,0:T(8,128)(2,1)S(1)}, bf16[128,512]{1,0:T(8,128)(2,1)}, u32[]{:S(2)}, u32[]{:S(2)}) %collective-permute-start.32) | collective-permute-done | bytes 131104 | tf_op jit(solution)/shard_map/ppermute | solution.py:44
  132.6 1.5 shard_map.93
  134.1 0.8 copy-done.12
  134.9 0.8 copy-done.18
  136.2 0.8 copy-done.20
  137.0 2.0 %collective-permute-start.53 = (bf16[128,1024]{1,0:T(8,128)(2,1)}, bf16[128,1024]{1,0:T(8,128)(2,1)}, u32[]{:S(2)}, u32[]{:S(2)}) collective-permute-start(bf16[128,1024]{1,0:T(8,128)(2,1)} %get-tuple-element.48), channel_id=1, source_target_pairs={{0,72},{1,73},{2,74},{3,75},{4,76},{5,77},{6,78},{7,79},{8,64},{9,... | collective-permute-start | bytes 786440 | tf_op jit(solution)/shard_map/ppermute | solution.py:40
  139.6 1.6 collective-permute-start.54
  141.3 1.0 copy-done.15
  142.3 1.0 copy-done.17
  143.3 1.0 copy-done.19
  144.4 1.0 copy-done.21
  145.4 0.9 copy-done.36
  146.3 0.9 copy-done.38
  147.2 0.9 copy-done.40
  148.1 2.6 %shard_map.91 = (f32[128,1024]{1,0:T(8,128)S(1)}, f32[144,1024]{1,0:T(8,128)S(1)}, f32[144,1024]{1,0:T(8,128)S(1)}, f32[144,1024]{1,0:T(8,128)S(1)}) custom-call(s32[1]{0:T(128)} %bitcast.core_ref, bf16[128,512]{1,0:T(8,128)(2,1)S(1)} %shard_map.90.refs_0_, bf16[128,512]{1,0:T(8,128)(2,1)S(1)} %copy-done.36, ...), custom_call_target="tpu_custom_call" | custom-call | flops 1073741824 | bytes 1048576 | tf_op jit(solution)/shard_map/pallas_call | solution.py:66
  150.9 0.8 copy-done.24
  151.7 2.7 %shard_map.92 = (f32[1024,256]{1,0:T(8,128)S(1)}, bf16[1024,256]{1,0:T(8,128)(2,1)S(1)}, bf16[1024,256]{1,0:T(8,128)(2,1)S(1)}, bf16[1024,256]{1,0:T(8,128)(2,1)S(1)}) custom-call(s32[1]{0:T(128)} %bitcast.core_ref, bf16[128,512]{1,0:T(8,128)(2,1)S(1)} %shard_map.90.refs_0_, bf16[128,512]{1,0:T(8,128)(2,1)} %collective-permute-done.32.refs_3_.refs_1_, ...), custom_call_target="tpu_custom_call" | custom-call | flops 1073741824 | bytes 1048576 | tf_op jit(solution)/shard_map/pallas_call | solution.py:66
  155.1 2.1 %collective-permute-start.47 = (bf16[1024,256]{1,0:T(8,128)(2,1)S(1)}, bf16[1024,256]{1,0:T(8,128)(2,1)S(1)}, u32[]{:S(2)}, u32[]{:S(2)}) collective-permute-start(bf16[1024,256]{1,0:T(8,128)(2,1)S(1)} %get-tuple-element.43), channel_id=1, source_target_pairs={{0,72},{1,73},{2,74},{3,75},{4,76},{5,77},{6,78},{7,79},{8,64},{9,... | collective-permute-start | bytes 1572872 | tf_op jit(solution)/shard_map/ppermute | solution.py:40
  157.2 1.6 collective-permute-start.48
  158.8 2.0 %convert_add_fusion = f32[128,1024]{1,0:T(8,128)} fusion(bf16[128,1024]{1,0:T(8,128)(2,1)} %collective-permute-done.54, bf16[128,1024]{1,0:T(8,128)(2,1)} %collective-permute-done.53, f32[128,1024]{1,0:T(8,128)S(1)} %copy-done.13, bf16[128,1024]{1,0:T(8,128)(2,1)} %collective-permute-done.52), kind=kLoop, calls=%fused_computation.7 | loop fusion | flops 786432 | bytes 1835008 | tf_op jit(solution)/shard_map/add | solution.py:314
  161.0 3.1 %collective-permute-start.42 = (f16[144,1024]{1,0:T(8,128)(2,1)S(1)}, f16[144,1024]{1,0:T(8,128)(2,1)S(1)}, u32[]{:S(2)}, u32[]{:S(2)}) collective-permute-start(f16[144,1024]{1,0:T(8,128)(2,1)S(1)} %convert_element_type.98), channel_id=1, source_target_pairs={{0,6},{2,0},{4,2},{6,4},{1,7},{3,1},{5,3},{7,5},{8,14},{10,8},{12,... | collective-permute-start | bytes 884744 | tf_op jit(solution)/shard_map/ppermute | solution.py:44
  164.2 3.7 %collective-permute-done.41 = f16[144,1024]{1,0:T(8,128)(2,1)S(1)} collective-permute-done((f16[144,1024]{1,0:T(8,128)(2,1)S(1)}, f16[144,1024]{1,0:T(8,128)(2,1)S(1)}, u32[]{:S(2)}, u32[]{:S(2)}) %collective-permute-start.41) | collective-permute-done | bytes 294944 | tf_op jit(solution)/shard_map/ppermute | solution.py:44
  168.0 1.2 collective-permute-done.42
  170.5 8.5 %collective-permute-done.47 = bf16[1024,256]{1,0:T(8,128)(2,1)S(1)} collective-permute-done((bf16[1024,256]{1,0:T(8,128)(2,1)S(1)}, bf16[1024,256]{1,0:T(8,128)(2,1)S(1)}, u32[]{:S(2)}, u32[]{:S(2)}) %collective-permute-start.47) | collective-permute-done | bytes 524320 | tf_op jit(solution)/shard_map/ppermute | solution.py:40
  179.0 3.5 %collective-permute-done.48 = bf16[1024,256]{1,0:T(8,128)(2,1)S(1)} collective-permute-done((bf16[1024,256]{1,0:T(8,128)(2,1)S(1)}, bf16[1024,256]{1,0:T(8,128)(2,1)S(1)}, u32[]{:S(2)}, u32[]{:S(2)}) %collective-permute-start.48) | collective-permute-done | bytes 524320 | tf_op jit(solution)/shard_map/ppermute | solution.py:40
  182.5 1.2 convert_add_fusion.1
  183.7 0.7 pad_maximum_fusion
  (177 shorter events, 14.7 us)
Async XLA Ops:
  0.6 7.4 %copy-start.41 = (bf16[256,512]{1,0:T(8,128)(2,1)S(1)}, bf16[256,512]{1,0:T(8,128)(2,1)}, u32[]{:S(2)}) copy-start(bf16[256,512]{1,0:T(8,128)(2,1)} %param.6) | copy-start | bytes 786436
  1.7 6.4 %collective-permute-start.15 = (bf16[128,512]{1,0:T(8,128)(2,1)S(1)}, bf16[128,512]{1,0:T(8,128)(2,1)S(1)}, u32[]{:S(2)}, u32[]{:S(2)}) collective-permute-start(bf16[128,512]{1,0:T(8,128)(2,1)S(1)} %get-tuple-element.57), channel_id=1, source_target_pairs={{0,0},{1,1},{2,18},{3,19},{4,36},{5,37},{6,54},{7,55},{8,8},{9,9},... | collective-permute-start | bytes 393224 | tf_op jit(solution)/shard_map/ppermute | solution.py:40
  2.4 6.4 %collective-permute-start.16 = (bf16[128,512]{1,0:T(8,128)(2,1)S(1)}, bf16[128,512]{1,0:T(8,128)(2,1)S(1)}, u32[]{:S(2)}, u32[]{:S(2)}) collective-permute-start(bf16[128,512]{1,0:T(8,128)(2,1)S(1)} %get-tuple-element.56), channel_id=1, source_target_pairs={{0,8},{1,9},{2,26},{3,27},{4,44},{5,45},{6,62},{7,63},{8,0},{9,1},... | collective-permute-start | bytes 393224 | tf_op jit(solution)/shard_map/ppermute | solution.py:40
  4.5 27.6 %collective-permute-start.10 = (bf16[128,1024]{1,0:T(8,128)(2,1)S(1)}, bf16[128,1024]{1,0:T(8,128)(2,1)S(1)}, u32[]{:S(2)}, u32[]{:S(2)}) collective-permute-start(bf16[128,1024]{1,0:T(8,128)(2,1)S(1)} %copy-done.27), channel_id=1, source_target_pairs={{0,64},{1,65},{2,66},{3,67},{4,68},{5,69},{6,70},{7,71},{8,72},{9,... | collective-permute-start | bytes 786440 | tf_op jit(solution)/shard_map/ppermute | solution.py:40
  8.1 24.8 %collective-permute-start.11 = (bf16[128,1024]{1,0:T(8,128)(2,1)S(1)}, bf16[128,1024]{1,0:T(8,128)(2,1)S(1)}, u32[]{:S(2)}, u32[]{:S(2)}) collective-permute-start(bf16[128,1024]{1,0:T(8,128)(2,1)S(1)} %copy-done.27), channel_id=1, source_target_pairs={{0,72},{1,73},{2,74},{3,75},{4,76},{5,77},{6,78},{7,79},{8,64},{9,... | collective-permute-start | bytes 786440 | tf_op jit(solution)/shard_map/ppermute | solution.py:40
  8.1 25.6 %collective-permute-start.9 = (bf16[128,1024]{1,0:T(8,128)(2,1)S(1)}, bf16[128,1024]{1,0:T(8,128)(2,1)S(1)}, u32[]{:S(2)}, u32[]{:S(2)}) collective-permute-start(bf16[128,1024]{1,0:T(8,128)(2,1)S(1)} %copy-done.27), channel_id=1, source_target_pairs={{0,8},{1,9},{2,10},{3,11},{4,12},{5,13},{6,14},{7,15},{8,0},{9,1},... | collective-permute-start | bytes 786440 | tf_op jit(solution)/shard_map/ppermute | solution.py:40
  8.1 2.8 %collective-permute-start = (bf16[128,512]{1,0:T(8,128)(2,1)S(1)}, bf16[128,512]{1,0:T(8,128)(2,1)S(1)}, u32[]{:S(2)}, u32[]{:S(2)}) collective-permute-start(bf16[128,512]{1,0:T(8,128)(2,1)S(1)} %get-tuple-element.59), channel_id=1, source_target_pairs={{0,0},{1,1},{2,18},{3,19},{4,36},{5,37},{6,54},{7,55},{8,8},{9,9},... | collective-permute-start | bytes 393224 | tf_op jit(solution)/shard_map/ppermute | solution.py:40
  8.8 13.3 %collective-permute-start.1 = (bf16[128,512]{1,0:T(8,128)(2,1)S(1)}, bf16[128,512]{1,0:T(8,128)(2,1)S(1)}, u32[]{:S(2)}, u32[]{:S(2)}) collective-permute-start(bf16[128,512]{1,0:T(8,128)(2,1)S(1)} %get-tuple-element.58), channel_id=1, source_target_pairs={{0,8},{1,9},{2,26},{3,27},{4,44},{5,45},{6,62},{7,63},{8,0},{9,1},... | collective-permute-start | bytes 393224 | tf_op jit(solution)/shard_map/ppermute | solution.py:40
  10.9 22.6 %copy-start.25 = (bf16[1024,128]{1,0:T(8,128)(2,1)S(1)}, bf16[1024,128]{1,0:T(8,128)(2,1)}, u32[]{:S(2)}) copy-start(bf16[1024,128]{1,0:T(8,128)(2,1)} %a_ref.1) | copy-start | bytes 786436
  10.9 22.6 %copy-start.26 = (bf16[1024,128]{1,0:T(8,128)(2,1)S(1)}, bf16[1024,128]{1,0:T(8,128)(2,1)}, u32[]{:S(2)}) copy-start(bf16[1024,128]{1,0:T(8,128)(2,1)} %b_ref.1) | copy-start | bytes 786436
  10.9 24.2 %collective-permute-start.17 = (bf16[128,1024]{1,0:T(8,128)(2,1)S(1)}, bf16[128,1024]{1,0:T(8,128)(2,1)}, u32[]{:S(2)}, u32[]{:S(2)}) collective-permute-start(bf16[128,1024]{1,0:T(8,128)(2,1)S(1)} %shard_map.86.refs_0_.refs_4_), channel_id=1, source_target_pairs={{0,2},{2,4},{4,6},{6,0},{1,3},{3,5},{5,7},{7,1},{8,10},{10,12},{12... | collective-permute-start | bytes 786440 | tf_op jit(solution)/shard_map/ppermute | solution.py:44
  22.1 15.2 %collective-permute-start.18 = (bf16[128,1024]{1,0:T(8,128)(2,1)S(1)}, bf16[128,1024]{1,0:T(8,128)(2,1)}, u32[]{:S(2)}, u32[]{:S(2)}) collective-permute-start(bf16[128,1024]{1,0:T(8,128)(2,1)S(1)} %shard_map.86.refs_0_.refs_4_), channel_id=1, source_target_pairs={{0,4},{2,6},{4,0},{6,2},{1,5},{3,7},{5,1},{7,3},{8,12},{10,14},{12... | collective-permute-start | bytes 786440 | tf_op jit(solution)/shard_map/ppermute | solution.py:44
  32.8 7.3 %collective-permute-start.19 = (bf16[128,1024]{1,0:T(8,128)(2,1)S(1)}, bf16[128,1024]{1,0:T(8,128)(2,1)}, u32[]{:S(2)}, u32[]{:S(2)}) collective-permute-start(bf16[128,1024]{1,0:T(8,128)(2,1)S(1)} %shard_map.86.refs_0_.refs_4_), channel_id=1, source_target_pairs={{0,6},{2,0},{4,2},{6,4},{1,7},{3,1},{5,3},{7,5},{8,14},{10,8},{12,... | collective-permute-start | bytes 786440 | tf_op jit(solution)/shard_map/ppermute | solution.py:44
  33.5 7.6 %collective-permute-start.20 = (bf16[128,1024]{1,0:T(8,128)(2,1)S(1)}, bf16[128,1024]{1,0:T(8,128)(2,1)S(1)}, u32[]{:S(2)}, u32[]{:S(2)}) collective-permute-start(bf16[128,1024]{1,0:T(8,128)(2,1)S(1)} %shard_map.86.refs_0_.refs_4_), channel_id=1, source_target_pairs={{0,1},{1,0},{2,3},{3,2},{4,5},{5,4},{6,7},{7,6},{8,9},{9,8},{10,11... | collective-permute-start | bytes 786440 | tf_op jit(solution)/shard_map/ppermute | solution.py:48
  33.7 21.7 %collective-permute-start.24 = (bf16[1024,256]{1,0:T(8,128)(2,1)S(1)}, bf16[1024,256]{1,0:T(8,128)(2,1)S(1)}, u32[]{:S(2)}, u32[]{:S(2)}) collective-permute-start(bf16[1024,256]{1,0:T(8,128)(2,1)S(1)} %shard_map.87.refs_8_), channel_id=1, source_target_pairs={{0,8},{1,9},{2,10},{3,11},{4,12},{5,13},{6,14},{7,15},{8,0},{9,1},... | collective-permute-start | bytes 1572872 | tf_op jit(solution)/shard_map/ppermute | solution.py:40
  35.2 15.3 %collective-permute-start.2 = (bf16[128,1024]{1,0:T(8,128)(2,1)S(1)}, bf16[128,1024]{1,0:T(8,128)(2,1)S(1)}, u32[]{:S(2)}, u32[]{:S(2)}) collective-permute-start(bf16[128,1024]{1,0:T(8,128)(2,1)S(1)} %shard_map.84.refs_0_.refs_4_), channel_id=1, source_target_pairs={{0,2},{2,4},{4,6},{6,0},{1,3},{3,5},{5,7},{7,1},{8,10},{10,12},{12... | collective-permute-start | bytes 786440 | tf_op jit(solution)/shard_map/ppermute | solution.py:44
  37.3 16.7 %collective-permute-start.3 = (bf16[128,1024]{1,0:T(8,128)(2,1)S(1)}, bf16[128,1024]{1,0:T(8,128)(2,1)S(1)}, u32[]{:S(2)}, u32[]{:S(2)}) collective-permute-start(bf16[128,1024]{1,0:T(8,128)(2,1)S(1)} %shard_map.84.refs_0_.refs_4_), channel_id=1, source_target_pairs={{0,4},{2,6},{4,0},{6,2},{1,5},{3,7},{5,1},{7,3},{8,12},{10,14},{12... | collective-permute-start | bytes 786440 | tf_op jit(solution)/shard_map/ppermute | solution.py:44
  40.1 13.9 %collective-permute-start.4 = (bf16[128,1024]{1,0:T(8,128)(2,1)S(1)}, bf16[128,1024]{1,0:T(8,128)(2,1)S(1)}, u32[]{:S(2)}, u32[]{:S(2)}) collective-permute-start(bf16[128,1024]{1,0:T(8,128)(2,1)S(1)} %shard_map.84.refs_0_.refs_4_), channel_id=1, source_target_pairs={{0,6},{2,0},{4,2},{6,4},{1,7},{3,1},{5,3},{7,5},{8,14},{10,8},{12,... | collective-permute-start | bytes 786440 | tf_op jit(solution)/shard_map/ppermute | solution.py:44
  41.8 12.3 %collective-permute-start.5 = (bf16[128,1024]{1,0:T(8,128)(2,1)S(1)}, bf16[128,1024]{1,0:T(8,128)(2,1)S(1)}, u32[]{:S(2)}, u32[]{:S(2)}) collective-permute-start(bf16[128,1024]{1,0:T(8,128)(2,1)S(1)} %shard_map.84.refs_0_.refs_4_), channel_id=1, source_target_pairs={{0,1},{1,0},{2,3},{3,2},{4,5},{5,4},{6,7},{7,6},{8,9},{9,8},{10,11... | collective-permute-start | bytes 786440 | tf_op jit(solution)/shard_map/ppermute | solution.py:48
  50.5 17.0 %collective-permute-start.25 = (bf16[1024,256]{1,0:T(8,128)(2,1)S(1)}, bf16[1024,256]{1,0:T(8,128)(2,1)S(1)}, u32[]{:S(2)}, u32[]{:S(2)}) collective-permute-start(bf16[1024,256]{1,0:T(8,128)(2,1)S(1)} %shard_map.87.refs_8_), channel_id=1, source_target_pairs={{0,64},{1,65},{2,66},{3,67},{4,68},{5,69},{6,70},{7,71},{8,72},{9,... | collective-permute-start | bytes 1572872 | tf_op jit(solution)/shard_map/ppermute | solution.py:40
  54.0 23.0 %collective-permute-start.26 = (bf16[1024,256]{1,0:T(8,128)(2,1)S(1)}, bf16[1024,256]{1,0:T(8,128)(2,1)S(1)}, u32[]{:S(2)}, u32[]{:S(2)}) collective-permute-start(bf16[1024,256]{1,0:T(8,128)(2,1)S(1)} %shard_map.87.refs_8_), channel_id=1, source_target_pairs={{0,72},{1,73},{2,74},{3,75},{4,76},{5,77},{6,78},{7,79},{8,64},{9,... | collective-permute-start | bytes 1572872 | tf_op jit(solution)/shard_map/ppermute | solution.py:40
  54.0 1.6 collective-permute-start.6
  54.8 1.7 collective-permute-start.7
  55.3 2.2 %collective-permute-start.8 = (bf16[128,1024]{1,0:T(8,128)(2,1)S(1)}, bf16[128,1024]{1,0:T(8,128)(2,1)S(1)}, u32[]{:S(2)}, u32[]{:S(2)}) collective-permute-start(bf16[128,1024]{1,0:T(8,128)(2,1)S(1)} %collective-permute-done.4.refs_3_.refs_7_), channel_id=1, source_target_pairs={{0,1},{1,0},{2,3},{3,2},{4,5},{5,4},{6,7},{7,6},{8,9},{9,8},{10,11... | collective-permute-start | bytes 786440 | tf_op jit(solution)/shard_map/ppermute | solution.py:48
  56.3 20.7 %collective-permute-start.21 = (bf16[128,1024]{1,0:T(8,128)(2,1)}, bf16[128,1024]{1,0:T(8,128)(2,1)}, u32[]{:S(2)}, u32[]{:S(2)}) collective-permute-start(bf16[128,1024]{1,0:T(8,128)(2,1)} %collective-permute-done.17.refs_1_.refs_5_), channel_id=1, source_target_pairs={{0,1},{1,0},{2,3},{3,2},{4,5},{5,4},{6,7},{7,6},{8,9},{9,8},{10,11... | collective-permute-start | bytes 786440 | tf_op jit(solution)/shard_map/ppermute | solution.py:48
  57.3 20.3 %collective-permute-start.22 = (bf16[128,1024]{1,0:T(8,128)(2,1)}, bf16[128,1024]{1,0:T(8,128)(2,1)}, u32[]{:S(2)}, u32[]{:S(2)}) collective-permute-start(bf16[128,1024]{1,0:T(8,128)(2,1)} %collective-permute-done.18.refs_2_.refs_6_), channel_id=1, source_target_pairs={{0,1},{1,0},{2,3},{3,2},{4,5},{5,4},{6,7},{7,6},{8,9},{9,8},{10,11... | collective-permute-start | bytes 786440 | tf_op jit(solution)/shard_map/ppermute | solution.py:48
  58.3 19.4 %collective-permute-start.23 = (bf16[128,1024]{1,0:T(8,128)(2,1)}, bf16[128,1024]{1,0:T(8,128)(2,1)}, u32[]{:S(2)}, u32[]{:S(2)}) collective-permute-start(bf16[128,1024]{1,0:T(8,128)(2,1)} %collective-permute-done.19.refs_3_.refs_7_), channel_id=1, source_target_pairs={{0,1},{1,0},{2,3},{3,2},{4,5},{5,4},{6,7},{7,6},{8,9},{9,8},{10,11... | collective-permute-start | bytes 786440 | tf_op jit(solution)/shard_map/ppermute | solution.py:48
  66.1 11.6 %copy-start.23 = (bf16[128,1024]{1,0:T(8,128)(2,1)S(1)}, bf16[128,1024]{1,0:T(8,128)(2,1)}, u32[]{:S(2)}) copy-start(bf16[128,1024]{1,0:T(8,128)(2,1)} %copy-done.22) | copy-start | bytes 786436
  67.5 47.0 %collective-permute-start.37 = (bf16[1024,256]{1,0:T(8,128)(2,1)S(1)}, bf16[1024,256]{1,0:T(8,128)(2,1)S(1)}, u32[]{:S(2)}, u32[]{:S(2)}) collective-permute-start(bf16[1024,256]{1,0:T(8,128)(2,1)S(1)} %shard_map.87.refs_8_), channel_id=1, source_target_pairs={{0,1},{1,0},{2,3},{3,2},{4,5},{5,4},{6,7},{7,6},{8,9},{9,8},{10,11... | collective-permute-start | bytes 1572872 | tf_op jit(solution)/shard_map/ppermute | solution.py:48
  77.0 55.4 %collective-permute-start.38 = (bf16[1024,256]{1,0:T(8,128)(2,1)S(1)}, bf16[1024,256]{1,0:T(8,128)(2,1)S(1)}, u32[]{:S(2)}, u32[]{:S(2)}) collective-permute-start(bf16[1024,256]{1,0:T(8,128)(2,1)S(1)} %collective-permute-done.24.refs_9_), channel_id=1, source_target_pairs={{0,1},{1,0},{2,3},{3,2},{4,5},{5,4},{6,7},{7,6},{8,9},{9,8},{10,11... | collective-permute-start | bytes 1572872 | tf_op jit(solution)/shard_map/ppermute | solution.py:48
  77.1 57.9 %collective-permute-start.39 = (bf16[1024,256]{1,0:T(8,128)(2,1)S(1)}, bf16[1024,256]{1,0:T(8,128)(2,1)S(1)}, u32[]{:S(2)}, u32[]{:S(2)}) collective-permute-start(bf16[1024,256]{1,0:T(8,128)(2,1)S(1)} %collective-permute-done.25.refs_10_), channel_id=1, source_target_pairs={{0,1},{1,0},{2,3},{3,2},{4,5},{5,4},{6,7},{7,6},{8,9},{9,8},{10,11... | collective-permute-start | bytes 1572872 | tf_op jit(solution)/shard_map/ppermute | solution.py:48
  77.6 58.6 %collective-permute-start.40 = (bf16[1024,256]{1,0:T(8,128)(2,1)S(1)}, bf16[1024,256]{1,0:T(8,128)(2,1)S(1)}, u32[]{:S(2)}, u32[]{:S(2)}) collective-permute-start(bf16[1024,256]{1,0:T(8,128)(2,1)S(1)} %collective-permute-done.26.refs_11_), channel_id=1, source_target_pairs={{0,1},{1,0},{2,3},{3,2},{4,5},{5,4},{6,7},{7,6},{8,9},{9,8},{10,11... | collective-permute-start | bytes 1572872 | tf_op jit(solution)/shard_map/ppermute | solution.py:48
  77.7 5.8 %collective-permute-start.12 = (f16[144,256]{1,0:T(8,128)(2,1)S(1)}, f16[144,256]{1,0:T(8,128)(2,1)S(1)}, u32[]{:S(2)}, u32[]{:S(2)}) collective-permute-start(f16[144,256]{1,0:T(8,128)(2,1)S(1)} %convert_element_type.84), channel_id=1, source_target_pairs={{0,16},{16,32},{32,48},{48,0},{1,17},{17,33},{33,49},{49,1},{2,18}... | collective-permute-start | bytes 221192 | tf_op jit(solution)/shard_map/ppermute | solution.py:44
  83.5 4.4 %collective-permute-start.13 = (f16[144,256]{1,0:T(8,128)(2,1)S(1)}, f16[144,256]{1,0:T(8,128)(2,1)S(1)}, u32[]{:S(2)}, u32[]{:S(2)}) collective-permute-start(f16[144,256]{1,0:T(8,128)(2,1)S(1)} %convert_element_type.86), channel_id=1, source_target_pairs={{0,48},{16,0},{32,16},{48,32},{1,49},{17,1},{33,17},{49,33},{2,50}... | collective-permute-start | bytes 221192 | tf_op jit(solution)/shard_map/ppermute | solution.py:44
  87.8 6.4 %collective-permute-start.27 = (f16[144,512]{1,0:T(8,128)(2,1)S(1)}, f16[144,512]{1,0:T(8,128)(2,1)S(1)}, u32[]{:S(2)}, u32[]{:S(2)}) collective-permute-start(f16[144,512]{1,0:T(8,128)(2,1)S(1)} %convert_element_type.90), channel_id=1, source_target_pairs={{0,16},{16,32},{32,48},{48,0},{1,17},{17,33},{33,49},{49,1},{2,18}... | collective-permute-start | bytes 442376 | tf_op jit(solution)/shard_map/ppermute | solution.py:44
  94.2 5.3 %collective-permute-start.28 = (f16[144,512]{1,0:T(8,128)(2,1)S(1)}, f16[144,512]{1,0:T(8,128)(2,1)S(1)}, u32[]{:S(2)}, u32[]{:S(2)}) collective-permute-start(f16[144,512]{1,0:T(8,128)(2,1)S(1)} %convert_element_type.92), channel_id=1, source_target_pairs={{0,48},{16,0},{32,16},{48,32},{1,49},{17,1},{33,17},{49,33},{2,50}... | collective-permute-start | bytes 442376 | tf_op jit(solution)/shard_map/ppermute | solution.py:44
  99.5 7.4 %collective-permute-start.29 = (f16[144,512]{1,0:T(8,128)(2,1)S(1)}, f16[144,512]{1,0:T(8,128)(2,1)S(1)}, u32[]{:S(2)}, u32[]{:S(2)}) collective-permute-start(f16[144,512]{1,0:T(8,128)(2,1)S(1)} %convert_element_type.94), channel_id=1, source_target_pairs={{0,32},{16,48},{32,0},{48,16},{1,33},{17,49},{33,1},{49,17},{2,34}... | collective-permute-start | bytes 442376 | tf_op jit(solution)/shard_map/ppermute | solution.py:44
  106.9 6.3 %collective-permute-start.14 = (f16[144,256]{1,0:T(8,128)(2,1)S(1)}, f16[144,256]{1,0:T(8,128)(2,1)S(1)}, u32[]{:S(2)}, u32[]{:S(2)}) collective-permute-start(f16[144,256]{1,0:T(8,128)(2,1)S(1)} %convert_element_type.88), channel_id=1, source_target_pairs={{0,32},{16,48},{32,0},{48,16},{1,33},{17,49},{33,1},{49,17},{2,34}... | collective-permute-start | bytes 221192 | tf_op jit(solution)/shard_map/ppermute | solution.py:44
  113.4 4.3 %collective-permute-start.49 = (bf16[128,256]{1,0:T(8,128)(2,1)S(1)}, bf16[128,256]{1,0:T(8,128)(2,1)S(1)}, u32[]{:S(2)}, u32[]{:S(2)}) collective-permute-start(bf16[128,256]{1,0:T(8,128)(2,1)S(1)} %get-tuple-element.45.refs_0_), channel_id=1, source_target_pairs={{0,48},{16,0},{32,16},{48,32},{1,49},{17,1},{33,17},{49,33},{2,50}... | collective-permute-start | bytes 196616 | tf_op jit(solution)/shard_map/ppermute | solution.py:44
  114.6 6.1 %collective-permute-start.50 = (bf16[128,256]{1,0:T(8,128)(2,1)S(1)}, bf16[128,256]{1,0:T(8,128)(2,1)S(1)}, u32[]{:S(2)}, u32[]{:S(2)}) collective-permute-start(bf16[128,256]{1,0:T(8,128)(2,1)S(1)} %get-tuple-element.45.refs_0_), channel_id=1, source_target_pairs={{0,32},{16,48},{32,0},{48,16},{1,33},{17,49},{33,1},{49,17},{2,34}... | collective-permute-start | bytes 196616 | tf_op jit(solution)/shard_map/ppermute | solution.py:44
  117.7 5.5 %collective-permute-start.51 = (bf16[128,256]{1,0:T(8,128)(2,1)S(1)}, bf16[128,256]{1,0:T(8,128)(2,1)S(1)}, u32[]{:S(2)}, u32[]{:S(2)}) collective-permute-start(bf16[128,256]{1,0:T(8,128)(2,1)S(1)} %get-tuple-element.45.refs_0_), channel_id=1, source_target_pairs={{0,16},{16,32},{32,48},{48,0},{1,17},{17,33},{33,49},{49,1},{2,18}... | collective-permute-start | bytes 196616 | tf_op jit(solution)/shard_map/ppermute | solution.py:44
  117.7 14.9 %copy-start.8 = (bf16[128,1024]{1,0:T(8,128)(2,1)S(1)}, bf16[128,1024]{1,0:T(8,128)(2,1)}, u32[]{:S(2)}) copy-start(bf16[128,1024]{1,0:T(8,128)(2,1)} %copy-done.6) | copy-start | bytes 786436
  117.7 14.9 %copy-start.11 = (bf16[128,1024]{1,0:T(8,128)(2,1)S(1)}, bf16[128,1024]{1,0:T(8,128)(2,1)}, u32[]{:S(2)}) copy-start(bf16[128,1024]{1,0:T(8,128)(2,1)} %copy-done.9) | copy-start | bytes 786436
  117.7 14.8 %copy-start.2 = (bf16[128,1024]{1,0:T(8,128)(2,1)S(1)}, bf16[128,1024]{1,0:T(8,128)(2,1)}, u32[]{:S(2)}) copy-start(bf16[128,1024]{1,0:T(8,128)(2,1)} %copy-done) | copy-start | bytes 786436
  117.8 14.8 %copy-start.5 = (bf16[128,1024]{1,0:T(8,128)(2,1)S(1)}, bf16[128,1024]{1,0:T(8,128)(2,1)}, u32[]{:S(2)}) copy-start(bf16[128,1024]{1,0:T(8,128)(2,1)} %copy-done.3) | copy-start | bytes 786436
  120.7 6.2 %collective-permute-start.30 = (bf16[128,512]{1,0:T(8,128)(2,1)S(1)}, bf16[128,512]{1,0:T(8,128)(2,1)S(1)}, u32[]{:S(2)}, u32[]{:S(2)}) collective-permute-start(bf16[128,512]{1,0:T(8,128)(2,1)S(1)} %shard_map.90.refs_0_), channel_id=1, source_target_pairs={{0,16},{16,32},{32,48},{48,0},{1,17},{17,33},{33,49},{49,1},{2,18}... | collective-permute-start | bytes 393224 | tf_op jit(solution)/shard_map/ppermute | solution.py:44
  123.2 6.6 %collective-permute-start.31 = (bf16[128,512]{1,0:T(8,128)(2,1)S(1)}, bf16[128,512]{1,0:T(8,128)(2,1)}, u32[]{:S(2)}, u32[]{:S(2)}) collective-permute-start(bf16[128,512]{1,0:T(8,128)(2,1)S(1)} %shard_map.90.refs_0_), channel_id=1, source_target_pairs={{0,32},{16,48},{32,0},{48,16},{1,33},{17,49},{33,1},{49,17},{2,34}... | collective-permute-start | bytes 393224 | tf_op jit(solution)/shard_map/ppermute | solution.py:44
  126.9 7.2 %copy-start.35 = (bf16[128,512]{1,0:T(8,128)(2,1)}, bf16[128,512]{1,0:T(8,128)(2,1)S(1)}, u32[]{:S(2)}) copy-start(bf16[128,512]{1,0:T(8,128)(2,1)S(1)} %collective-permute-done.30.refs_1_.refs_3_) | copy-start | bytes 393220
  126.9 5.1 %collective-permute-start.32 = (bf16[128,512]{1,0:T(8,128)(2,1)S(1)}, bf16[128,512]{1,0:T(8,128)(2,1)}, u32[]{:S(2)}, u32[]{:S(2)}) collective-permute-start(bf16[128,512]{1,0:T(8,128)(2,1)S(1)} %shard_map.90.refs_0_), channel_id=1, source_target_pairs={{0,48},{16,0},{32,16},{48,32},{1,49},{17,1},{33,17},{49,33},{2,50}... | collective-permute-start | bytes 393224 | tf_op jit(solution)/shard_map/ppermute | solution.py:44
  129.7 2.2 %collective-permute-start.33 = (bf16[128,512]{1,0:T(8,128)(2,1)S(1)}, bf16[128,512]{1,0:T(8,128)(2,1)S(1)}, u32[]{:S(2)}, u32[]{:S(2)}) collective-permute-start(bf16[128,512]{1,0:T(8,128)(2,1)S(1)} %shard_map.90.refs_0_), channel_id=1, source_target_pairs={{0,1},{1,0},{2,3},{3,2},{4,5},{5,4},{6,7},{7,6},{8,9},{9,8},{10,11... | collective-permute-start | bytes 393224 | tf_op jit(solution)/shard_map/ppermute | solution.py:48
  132.0 7.0 %collective-permute-start.34 = (bf16[128,512]{1,0:T(8,128)(2,1)S(1)}, bf16[128,512]{1,0:T(8,128)(2,1)S(1)}, u32[]{:S(2)}, u32[]{:S(2)}) collective-permute-start(bf16[128,512]{1,0:T(8,128)(2,1)S(1)} %collective-permute-done.30.refs_1_.refs_3_), channel_id=1, source_target_pairs={{0,1},{1,0},{2,3},{3,2},{4,5},{5,4},{6,7},{7,6},{8,9},{9,8},{10,11... | collective-permute-start | bytes 393224 | tf_op jit(solution)/shard_map/ppermute | solution.py:48
  132.0 9.3 %collective-permute-start.35 = (bf16[128,512]{1,0:T(8,128)(2,1)}, bf16[128,512]{1,0:T(8,128)(2,1)}, u32[]{:S(2)}, u32[]{:S(2)}) collective-permute-start(bf16[128,512]{1,0:T(8,128)(2,1)} %collective-permute-done.31.refs_2_), channel_id=1, source_target_pairs={{0,1},{1,0},{2,3},{3,2},{4,5},{5,4},{6,7},{7,6},{8,9},{9,8},{10,11... | collective-permute-start | bytes 393224 | tf_op jit(solution)/shard_map/ppermute | solution.py:48
  132.5 8.8 %collective-permute-start.36 = (bf16[128,512]{1,0:T(8,128)(2,1)}, bf16[128,512]{1,0:T(8,128)(2,1)}, u32[]{:S(2)}, u32[]{:S(2)}) collective-permute-start(bf16[128,512]{1,0:T(8,128)(2,1)} %collective-permute-done.32.refs_3_.refs_1_), channel_id=1, source_target_pairs={{0,1},{1,0},{2,3},{3,2},{4,5},{5,4},{6,7},{7,6},{8,9},{9,8},{10,11... | collective-permute-start | bytes 393224 | tf_op jit(solution)/shard_map/ppermute | solution.py:48
  135.7 19.4 %collective-permute-start.52 = (bf16[128,1024]{1,0:T(8,128)(2,1)}, bf16[128,1024]{1,0:T(8,128)(2,1)}, u32[]{:S(2)}, u32[]{:S(2)}) collective-permute-start(bf16[128,1024]{1,0:T(8,128)(2,1)} %get-tuple-element.47), channel_id=1, source_target_pairs={{0,8},{1,9},{2,10},{3,11},{4,12},{5,13},{6,14},{7,15},{8,0},{9,1},... | collective-permute-start | bytes 786440 | tf_op jit(solution)/shard_map/ppermute | solution.py:40
  137.0 20.3 %collective-permute-start.53 = (bf16[128,1024]{1,0:T(8,128)(2,1)}, bf16[128,1024]{1,0:T(8,128)(2,1)}, u32[]{:S(2)}, u32[]{:S(2)}) collective-permute-start(bf16[128,1024]{1,0:T(8,128)(2,1)} %get-tuple-element.48), channel_id=1, source_target_pairs={{0,72},{1,73},{2,74},{3,75},{4,76},{5,77},{6,78},{7,79},{8,64},{9,... | collective-permute-start | bytes 786440 | tf_op jit(solution)/shard_map/ppermute | solution.py:40
  139.6 19.2 %collective-permute-start.54 = (bf16[128,1024]{1,0:T(8,128)(2,1)}, bf16[128,1024]{1,0:T(8,128)(2,1)}, u32[]{:S(2)}, u32[]{:S(2)}) collective-permute-start(bf16[128,1024]{1,0:T(8,128)(2,1)} %get-tuple-element.49), channel_id=1, source_target_pairs={{0,64},{1,65},{2,66},{3,67},{4,68},{5,69},{6,70},{7,71},{8,72},{9,... | collective-permute-start | bytes 786440 | tf_op jit(solution)/shard_map/ppermute | solution.py:40
  150.8 10.2 %collective-permute-start.43 = (f16[144,1024]{1,0:T(8,128)(2,1)S(1)}, f16[144,1024]{1,0:T(8,128)(2,1)S(1)}, u32[]{:S(2)}, u32[]{:S(2)}) collective-permute-start(f16[144,1024]{1,0:T(8,128)(2,1)S(1)} %convert_element_type.100), channel_id=1, source_target_pairs={{0,4},{2,6},{4,0},{6,2},{1,5},{3,7},{5,1},{7,3},{8,12},{10,14},{12... | collective-permute-start | bytes 884744 | tf_op jit(solution)/shard_map/ppermute | solution.py:44
  154.5 16.1 %collective-permute-start.46 = (bf16[1024,256]{1,0:T(8,128)(2,1)S(1)}, bf16[1024,256]{1,0:T(8,128)(2,1)S(1)}, u32[]{:S(2)}, u32[]{:S(2)}) collective-permute-start(bf16[1024,256]{1,0:T(8,128)(2,1)S(1)} %get-tuple-element.42), channel_id=1, source_target_pairs={{0,8},{1,9},{2,10},{3,11},{4,12},{5,13},{6,14},{7,15},{8,0},{9,1},... | collective-permute-start | bytes 1572872 | tf_op jit(solution)/shard_map/ppermute | solution.py:40
  155.1 23.9 %collective-permute-start.47 = (bf16[1024,256]{1,0:T(8,128)(2,1)S(1)}, bf16[1024,256]{1,0:T(8,128)(2,1)S(1)}, u32[]{:S(2)}, u32[]{:S(2)}) collective-permute-start(bf16[1024,256]{1,0:T(8,128)(2,1)S(1)} %get-tuple-element.43), channel_id=1, source_target_pairs={{0,72},{1,73},{2,74},{3,75},{4,76},{5,77},{6,78},{7,79},{8,64},{9,... | collective-permute-start | bytes 1572872 | tf_op jit(solution)/shard_map/ppermute | solution.py:40
  157.2 25.3 %collective-permute-start.48 = (bf16[1024,256]{1,0:T(8,128)(2,1)S(1)}, bf16[1024,256]{1,0:T(8,128)(2,1)S(1)}, u32[]{:S(2)}, u32[]{:S(2)}) collective-permute-start(bf16[1024,256]{1,0:T(8,128)(2,1)S(1)} %get-tuple-element.44), channel_id=1, source_target_pairs={{0,64},{1,65},{2,66},{3,67},{4,68},{5,69},{6,70},{7,71},{8,72},{9,... | collective-permute-start | bytes 1572872 | tf_op jit(solution)/shard_map/ppermute | solution.py:40
  158.8 9.1 %collective-permute-start.41 = (f16[144,1024]{1,0:T(8,128)(2,1)S(1)}, f16[144,1024]{1,0:T(8,128)(2,1)S(1)}, u32[]{:S(2)}, u32[]{:S(2)}) collective-permute-start(f16[144,1024]{1,0:T(8,128)(2,1)S(1)} %convert_element_type.96), channel_id=1, source_target_pairs={{0,2},{2,4},{4,6},{6,0},{1,3},{3,5},{5,7},{7,1},{8,10},{10,12},{12... | collective-permute-start | bytes 884744 | tf_op jit(solution)/shard_map/ppermute | solution.py:44
  161.0 8.2 %collective-permute-start.42 = (f16[144,1024]{1,0:T(8,128)(2,1)S(1)}, f16[144,1024]{1,0:T(8,128)(2,1)S(1)}, u32[]{:S(2)}, u32[]{:S(2)}) collective-permute-start(f16[144,1024]{1,0:T(8,128)(2,1)S(1)} %convert_element_type.98), channel_id=1, source_target_pairs={{0,6},{2,0},{4,2},{6,4},{1,7},{3,1},{5,3},{7,5},{8,14},{10,8},{12,... | collective-permute-start | bytes 884744 | tf_op jit(solution)/shard_map/ppermute | solution.py:44
  169.5 14.1 %collective-permute-start.44 = (bf16[128,512]{1,0:T(8,128)(2,1)S(1)}, bf16[128,512]{1,0:T(8,128)(2,1)S(1)}, u32[]{:S(2)}, u32[]{:S(2)}) collective-permute-start(bf16[128,512]{1,0:T(8,128)(2,1)S(1)} %get-tuple-element.54), channel_id=1, source_target_pairs={{0,0},{1,1},{18,2},{19,3},{36,4},{37,5},{54,6},{55,7},{8,8},{9,9},... | collective-permute-start | bytes 393224 | tf_op jit(solution)/shard_map/ppermute | solution.py:40
  170.2 13.5 %collective-permute-start.45 = (bf16[128,512]{1,0:T(8,128)(2,1)S(1)}, bf16[128,512]{1,0:T(8,128)(2,1)S(1)}, u32[]{:S(2)}, u32[]{:S(2)}) collective-permute-start(bf16[128,512]{1,0:T(8,128)(2,1)S(1)} %get-tuple-element.55), channel_id=1, source_target_pairs={{8,0},{9,1},{26,2},{27,3},{44,4},{45,5},{62,6},{63,7},{0,8},{1,9},... | collective-permute-start | bytes 393224 | tf_op jit(solution)/shard_map/ppermute | solution.py:40
  (33 other events, 39.6 us)
where the time goes:
time: 185 us; the launch traced here: 184 us
  waiting for transfers between devices  82.7 us (45%)
  starting transfers between devices  59.9 us (32%)
  local copies, waits for them, and re-layouts  24.4 us (13%)
  Pallas kernels  11.3 us (6%)
  other arithmetic  4.87 us (3%)
    ppermute x21, waiting for transfers between devices, turned(): return lax.ppermute(value, axis, [(i, (i + step) % 4) for i in range(4)])  60.8 us
    ppermute x21, starting transfers between devices, turned(): return lax.ppermute(value, axis, [(i, (i + step) % 4) for i in range(4)])  33.6 us
    ppermute x18, starting transfers between devices, moved(): return lax.ppermute(value, AXES, pairs)  23.4 us
    unnamed x84, local copies, waits for them, and re-layouts  23.3 us
    ppermute x18, waiting for transfers between devices, moved(): return lax.ppermute(value, AXES, pairs)  21.6 us
    pallas_call x10, Pallas kernels, call(): pl.pallas_call(body, in_specs=[smem] * len(scalars) + [vmem] * len(arrays...  11.3 us
  transfers between devices with their start and end apart: 55, of which 21 were waited for; matrix products, arithmetic and copies ran while one was open for 2% of the time, Pallas kernels for 6%

commit v1 on v0

--- a/solution.py
+++ b/solution.py
@@ -77,18 +77,34 @@
     return lax.dot_general(a, b, (((da,), (db,)), ((), ())), preferred_element_type=F32)
 
 
-def pack_kernel(flag_ref, p_ref, q_ref, out_ref):
+CORE, UNEVEN, LOW = 0, 1, 2
+
+
+def ordered_copy(swap, first, second, left, right):
+    @pl.when(swap == 0)
+    def _():
+        left[...] = first[...]
+        right[...] = second[...]
+
+    @pl.when(swap != 0)
+    def _():
+        left[...] = second[...]
+        right[...] = first[...]
+
+
+def pack_kernel(flags, p_ref, q_ref, out_ref):
     wide = p_ref.shape[1]
-
-    @pl.when(flag_ref[0] == 0)
-    def _():
-        out_ref[:, :wide] = p_ref[...]
-        out_ref[:, wide:] = q_ref[...]
-
-    @pl.when(flag_ref[0] != 0)
-    def _():
-        out_ref[:, :wide] = q_ref[...]
-        out_ref[:, wide:] = p_ref[...]
+    ordered_copy(flags[UNEVEN], p_ref, q_ref, out_ref.at[:, :wide], out_ref.at[:, wide:])
+
+
+def unpack_kernel(flags, in_ref, kept_ref, sent_ref):
+    wide = kept_ref.shape[1]
+    ordered_copy(flags[UNEVEN], in_ref.at[:, :wide], in_ref.at[:, wide:], kept_ref, sent_ref)
+
+
+def merge_kernel(flags, kept_ref, sent_ref, out_ref):
+    rows = kept_ref.shape[0]
+    ordered_copy(flags[LOW], kept_ref, sent_ref, out_ref.at[:rows], out_ref.at[rows:])
 
 
 def join_kernel(a_ref, b_ref, out_ref):
@@ -118,7 +134,7 @@
 
 def forward_kernel(core_ref, *refs, transposed, kinds):
     own, other, weights, outs = refs[:4], refs[4:8], refs[8:12], refs[12:16]
-    core = core_ref[0]
+    core = core_ref[CORE]
     half = own[0].shape[0]
     deep = own[0].shape[1] // 2
     totals = [None, None]
@@ -166,7 +182,7 @@
 
 def down_grad_kernel(core_ref, *refs, factor):
     hidden, own, other, outs = refs[:4], refs[4:8], refs[8:12], refs[12:16]
-    core = core_ref[0]
+    core = core_ref[CORE]
     deep = own[0].shape[1] // 2
     units = hidden[0].shape[1] // 2
     left = stacked(hidden, slice(None))
@@ -181,7 +197,7 @@
 
 def gate_up_grad_kernel(core_ref, *refs, factor):
     deltas, own, other, outs = refs[:4], refs[4:8], refs[8:12], refs[12:16]
-    core = core_ref[0]
+    core = core_ref[CORE]
     deep = own[0].shape[1] // 2
     right = [delta_columns(deltas, b) for b in (0, 1)]
     for side, rows in ((core, own), (1 - core, other)):
@@ -197,7 +213,7 @@
     deltas, weights, outs = (refs[:4], refs[4:8]), (refs[8:12], refs[12:16]), refs[16:20]
     half = deltas[0][0].shape[0]
     deep = weights[0][0].shape[0] // 2
-    at = pl.ds(pl.multiple_of(core_ref[0] * deep, deep), deep)
+    at = pl.ds(pl.multiple_of(core_ref[CORE] * deep, deep), deep)
     left = [[delta_columns(deltas[side], b) for b in (0, 1)] for side in (0, 1)]
     pieces = []
     for a in (0, 1):
@@ -217,15 +233,14 @@
     deep = gate_weight.shape[0] // 2
     units = gate_weight.shape[1]
     width = 2 * units
-    uneven = (zh ^ zl).reshape(1)
-    core = c.reshape(1)
     wide = 2 * deep
+    flags = jnp.stack([c, zh ^ zl, zl]).astype(jnp.int32)
 
     def to_block(value):
         mine = lax.dynamic_slice_in_dim(value, zl * half, half, 0)
         theirs = lax.dynamic_slice_in_dim(value, (1 - zl) * half, half, 0)
         p, q = moved(mine, stay), moved(theirs, cross)
-        return call(pack_kernel, [uneven], [p, q], [((half, wide), tokens.dtype)], 1000)[0]
+        return call(pack_kernel, [flags], [p, q], [((half, wide), tokens.dtype)], 1000)[0]
 
     def over_x(block):
         rows = {0: block}
@@ -253,11 +268,11 @@
 
     gu_flops = 2 * 4 * half * 4 * deep * 2 * width
     gu_parts = call(
-        functools.partial(forward_kernel, transposed=False, kinds=2), [core],
+        functools.partial(forward_kernel, transposed=False, kinds=2), [flags],
         [*x_own, *x_other, *gu], parts_of(2 * width), gu_flops,
     )
     down_parts = call(
-        functools.partial(forward_kernel, transposed=True, kinds=1), [core],
+        functools.partial(forward_kernel, transposed=True, kinds=1), [flags],
         [*g_own, *g_other, *down], parts_of(width), gu_flops // 2,
     )
 
@@ -291,16 +306,16 @@
         return [rows[0], rows[3], rows[2], rows[1]]
 
     down_out = call(
-        functools.partial(down_grad_kernel, factor=factor), [core],
+        functools.partial(down_grad_kernel, factor=factor), [flags],
         [*matching(hidden_rows), *g_own, *g_other],
         [((units, wide), F32)] + [((units, wide), BF16)] * 3, gu_flops // 2,
     )
     ig_parts = call(
-        input_grad_kernel, [core], [*delta_rows, *delta_other, *gu, *gu_other],
+        input_grad_kernel, [flags], [*delta_rows, *delta_other, *gu, *gu_other],
         parts_of(wide), gu_flops,
     )
     gu_out = call(
-        functools.partial(gate_up_grad_kernel, factor=factor), [core],
+        functools.partial(gate_up_grad_kernel, factor=factor), [flags],
         [*matching(delta_rows), *x_own, *x_other],
         [((wide, width), F32)] + [((wide, width), BF16)] * 3, gu_flops,
     )
@@ -319,10 +334,9 @@
     gate_grad, up_grad = total_of(gu_terms, slice(0, units)), total_of(gu_terms, slice(units, width))
 
     total = summed(ig_parts, "x").astype(BF16)
-    kept = jnp.where(zh == zl, total[:, :deep], total[:, deep:])
-    sent = jnp.where(zh == zl, total[:, deep:], total[:, :deep])
+    kept, sent = call(unpack_kernel, [flags], [total], [((half, deep), BF16)] * 2, 1000)
     kept, sent = moved(kept, stay, back=True), moved(sent, cross, back=True)
-    input_grad = jnp.concatenate([jnp.where(zl == 0, kept, sent), jnp.where(zl == 0, sent, kept)], axis=0)
+    input_grad = call(merge_kernel, [flags], [kept, sent], [((2 * half, deep), BF16)], 1000)[0]
     return (input_grad, gate_grad, up_grad, down_grad)
 
 

time: 185 us -> 190 us (1.027)
  waiting for transfers between devices: 82.7 us -> 112 us
  local copies, waits for them, and re-layouts: 24.4 us -> 1.09 us
    unnamed x84 -> x8, local copies, waits for them, and re-layouts: 23.3 us -> 0.02 us
    ppermute x18, waiting for transfers between devices: 21.6 us -> 38 us  [moved(): return lax.ppermute(value, AXES, pairs)]
    ppermute x21, waiting for transfers between devices: 60.8 us -> 71.1 us  [turned(): return lax.ppermute(value, axis, [(i, (i + step) % 4) for i in range(4)])]
    ppermute x16, waiting for transfers between devices: 0.33 us -> 2.67 us  [other_core(): return lax.ppermute(value, 'c', [(0, 1), (1, 0)])]
    pallas_call x10 -> x12, Pallas kernels: 11.3 us -> 12.3 us  [call(): pl.pallas_call(body, in_specs=[smem] * len(scalars) + [vmem] * len(arrays...]
  transfers between devices with their start and end apart: 55 -> 55, of which waited for: 21 -> 25; matrix products, arithmetic and copies ran while one was open for 2% -> 2% of each run, Pallas kernels for 6% -> 5%
where the time goes in v1:
time: 190 us
  waiting for transfers between devices  112 us (59%)
  starting transfers between devices  60.3 us (32%)
  Pallas kernels  12.3 us (6%)
  other arithmetic  3.08 us (2%)
    ppermute x21, waiting for transfers between devices, turned(): return lax.ppermute(value, axis, [(i, (i + step) % 4) for i in range(4)])  71.1 us
    ppermute x18, waiting for transfers between devices, moved(): return lax.ppermute(value, AXES, pairs)  38 us
    ppermute x21, starting transfers between devices, turned(): return lax.ppermute(value, axis, [(i, (i + step) % 4) for i in range(4)])  33.4 us
    ppermute x18, starting transfers between devices, moved(): return lax.ppermute(value, AXES, pairs)  24.4 us
    pallas_call x12, Pallas kernels, call(): pl.pallas_call(body, in_specs=[smem] * len(scalars) + [vmem] * len(arrays...  12.3 us
  transfers between devices with their start and end apart: 55, of which 25 were waited for; matrix products, arithmetic and copies ran while one was open for 2% of the time, Pallas kernels for 5%

profile of v1, /device:TPU:0, one launch (start us, length us, event | category | flops | bytes accessed | tf_op | source)
XLA Modules:
  0.0 189.7 jit_solution(13970979080063058971)
XLA Ops:
  0.7 1.0 constant_dynamic-slice_fusion
  1.7 0.7 collective-permute-start.15
  2.4 2.1 %collective-permute-start.16 = (bf16[128,512]{1,0:T(8,128)(2,1)S(1)}, bf16[128,512]{1,0:T(8,128)(2,1)S(1)}, u32[]{:S(2)}, u32[]{:S(2)}) collective-permute-start(bf16[128,512]{1,0:T(8,128)(2,1)S(1)} %get-tuple-element.56), channel_id=1, source_target_pairs={{0,8},{1,9},{2,26},{3,27},{4,44},{5,45},{6,62},{7,63},{8,0},{9,1},... | collective-permute-start | bytes 393224 | tf_op jit(solution)/shard_map/ppermute | solution.py:40
  4.5 3.6 %collective-permute-start.10 = (bf16[128,1024]{1,0:T(8,128)(2,1)S(1)}, bf16[128,1024]{1,0:T(8,128)(2,1)S(1)}, u32[]{:S(2)}, u32[]{:S(2)}) collective-permute-start(bf16[128,1024]{1,0:T(8,128)(2,1)S(1)} %copy-done.2), channel_id=1, source_target_pairs={{0,64},{1,65},{2,66},{3,67},{4,68},{5,69},{6,70},{7,71},{8,72},{9,... | collective-permute-start | bytes 786440 | tf_op jit(solution)/shard_map/ppermute | solution.py:40
  8.1 0.7 collective-permute-start
  8.8 2.1 %collective-permute-start.1 = (bf16[128,512]{1,0:T(8,128)(2,1)S(1)}, bf16[128,512]{1,0:T(8,128)(2,1)S(1)}, u32[]{:S(2)}, u32[]{:S(2)}) collective-permute-start(bf16[128,512]{1,0:T(8,128)(2,1)S(1)} %get-tuple-element.58), channel_id=1, source_target_pairs={{0,8},{1,9},{2,26},{3,27},{4,44},{5,45},{6,62},{7,63},{8,0},{9,1},... | collective-permute-start | bytes 393224 | tf_op jit(solution)/shard_map/ppermute | solution.py:40
  11.0 0.6 shard_map.86.refs_0_.refs_4_
  11.6 10.7 %collective-permute-start.17 = (bf16[128,1024]{1,0:T(8,128)(2,1)S(1)}, bf16[128,1024]{1,0:T(8,128)(2,1)S(1)}, u32[]{:S(2)}, u32[]{:S(2)}) collective-permute-start(bf16[128,1024]{1,0:T(8,128)(2,1)S(1)} %shard_map.86.refs_0_.refs_4_), channel_id=1, source_target_pairs={{0,2},{2,4},{4,6},{6,0},{1,3},{3,5},{5,7},{7,1},{8,10},{10,12},{12... | collective-permute-start | bytes 786440 | tf_op jit(solution)/shard_map/ppermute | solution.py:44
  22.2 9.9 %collective-permute-start.18 = (bf16[128,1024]{1,0:T(8,128)(2,1)S(1)}, bf16[128,1024]{1,0:T(8,128)(2,1)S(1)}, u32[]{:S(2)}, u32[]{:S(2)}) collective-permute-start(bf16[128,1024]{1,0:T(8,128)(2,1)S(1)} %shard_map.86.refs_0_.refs_4_), channel_id=1, source_target_pairs={{0,4},{2,6},{4,0},{6,2},{1,5},{3,7},{5,1},{7,3},{8,12},{10,14},{12... | collective-permute-start | bytes 786440 | tf_op jit(solution)/shard_map/ppermute | solution.py:44
  32.3 1.5 collective-permute-start.24
  33.8 0.6 shard_map.84.refs_0_.refs_4_
  34.4 2.0 %collective-permute-start.2 = (bf16[128,1024]{1,0:T(8,128)(2,1)S(1)}, bf16[128,1024]{1,0:T(8,128)(2,1)S(1)}, u32[]{:S(2)}, u32[]{:S(2)}) collective-permute-start(bf16[128,1024]{1,0:T(8,128)(2,1)S(1)} %shard_map.84.refs_0_.refs_4_), channel_id=1, source_target_pairs={{0,2},{2,4},{4,6},{6,0},{1,3},{3,5},{5,7},{7,1},{8,10},{10,12},{12... | collective-permute-start | bytes 786440 | tf_op jit(solution)/shard_map/ppermute | solution.py:44
  36.4 0.3 collective-permute-done.18.refs_2_.refs_6_
  36.7 3.3 %collective-permute-start.3 = (bf16[128,1024]{1,0:T(8,128)(2,1)S(1)}, bf16[128,1024]{1,0:T(8,128)(2,1)S(1)}, u32[]{:S(2)}, u32[]{:S(2)}) collective-permute-start(bf16[128,1024]{1,0:T(8,128)(2,1)S(1)} %shard_map.84.refs_0_.refs_4_), channel_id=1, source_target_pairs={{0,4},{2,6},{4,0},{6,2},{1,5},{3,7},{5,1},{7,3},{8,12},{10,14},{12... | collective-permute-start | bytes 786440 | tf_op jit(solution)/shard_map/ppermute | solution.py:44
  40.0 0.9 collective-permute-start.4
  41.0 8.7 %collective-permute-done.2.refs_1_.refs_5_ = bf16[128,1024]{1,0:T(8,128)(2,1)S(1)} collective-permute-done((bf16[128,1024]{1,0:T(8,128)(2,1)S(1)}, bf16[128,1024]{1,0:T(8,128)(2,1)S(1)}, u32[]{:S(2)}, u32[]{:S(2)}) %collective-permute-start.2) | collective-permute-done | bytes 262176 | tf_op jit(solution)/shard_map/ppermute | solution.py:44
  49.7 4.3 %collective-permute-start.25 = (bf16[1024,256]{1,0:T(8,128)(2,1)S(1)}, bf16[1024,256]{1,0:T(8,128)(2,1)S(1)}, u32[]{:S(2)}, u32[]{:S(2)}) collective-permute-start(bf16[1024,256]{1,0:T(8,128)(2,1)S(1)} %shard_map.87.refs_8_), channel_id=1, source_target_pairs={{0,64},{1,65},{2,66},{3,67},{4,68},{5,69},{6,70},{7,71},{8,72},{9,... | collective-permute-start | bytes 1572872 | tf_op jit(solution)/shard_map/ppermute | solution.py:40
  54.2 0.5 collective-permute-start.7
  54.8 0.9 collective-permute-done.6.refs_5_.refs_9_
  55.8 0.2 collective-permute-done.7.refs_6_.refs_10_
  56.2 0.2 collective-permute-done.8.refs_7_.refs_11_
  56.6 2.0 %shard_map.85 = (f32[128,256]{1,0:T(8,128)S(1)}, f32[144,256]{1,0:T(8,128)S(1)}, f32[144,256]{1,0:T(8,128)S(1)}, f32[144,256]{1,0:T(8,128)S(1)}) custom-call(s32[3]{0:T(128)S(1)} %pad_add_fusion.flags.core_ref, bf16[128,1024]{1,0:T(8,128)(2,1)S(1)} %shard_map.84.refs_0_.refs_4_, bf16[128,1024]{1,0:T(8,128)(2,1)S(1)} %collective-permute-done.2.refs_1_.refs_5_, ...), custom_call_target="tpu_custom_call" | custom-call | flops 536870912 | bytes 1048576 | tf_op jit(solution)/shard_map/pallas_call | solution.py:66
  58.6 7.4 %collective-permute-done.25.refs_10_ = bf16[1024,256]{1,0:T(8,128)(2,1)S(1)} collective-permute-done((bf16[1024,256]{1,0:T(8,128)(2,1)S(1)}, bf16[1024,256]{1,0:T(8,128)(2,1)S(1)}, u32[]{:S(2)}, u32[]{:S(2)}) %collective-permute-start.25) | collective-permute-done | bytes 524320 | tf_op jit(solution)/shard_map/ppermute | solution.py:40
  66.0 11.1 %collective-permute-done.26.refs_11_ = bf16[1024,256]{1,0:T(8,128)(2,1)S(1)} collective-permute-done((bf16[1024,256]{1,0:T(8,128)(2,1)S(1)}, bf16[1024,256]{1,0:T(8,128)(2,1)S(1)}, u32[]{:S(2)}, u32[]{:S(2)}) %collective-permute-start.26) | collective-permute-done | bytes 524320 | tf_op jit(solution)/shard_map/ppermute | solution.py:40
  77.1 0.5 collective-permute-start.39
  77.7 2.0 %shard_map.88 = (f32[128,512]{1,0:T(8,128)S(1)}, f32[144,512]{1,0:T(8,128)S(1)}, f32[144,512]{1,0:T(8,128)S(1)}, f32[144,512]{1,0:T(8,128)S(1)}) custom-call(s32[3]{0:T(128)S(1)} %pad_add_fusion.flags.core_ref, bf16[128,1024]{1,0:T(8,128)(2,1)S(1)} %shard_map.86.refs_0_.refs_4_, bf16[128,1024]{1,0:T(8,128)(2,1)S(1)} %collective-permute-done.17.refs_1_.refs_5_, ...), custom_call_target="tpu_custom_call" | custom-call | flops 1073741824 | bytes 1048576 | tf_op jit(solution)/shard_map/pallas_call | solution.py:66
  79.9 3.6 %collective-permute-done.12 = f16[144,256]{1,0:T(8,128)(2,1)S(1)} collective-permute-done((f16[144,256]{1,0:T(8,128)(2,1)S(1)}, f16[144,256]{1,0:T(8,128)(2,1)S(1)}, u32[]{:S(2)}, u32[]{:S(2)}) %collective-permute-start.12) | collective-permute-done | bytes 73760 | tf_op jit(solution)/shard_map/ppermute | solution.py:44
  83.6 4.3 %collective-permute-done.13 = f16[144,256]{1,0:T(8,128)(2,1)S(1)} collective-permute-done((f16[144,256]{1,0:T(8,128)(2,1)S(1)}, f16[144,256]{1,0:T(8,128)(2,1)S(1)}, u32[]{:S(2)}, u32[]{:S(2)}) %collective-permute-start.13) | collective-permute-done | bytes 73760 | tf_op jit(solution)/shard_map/ppermute | solution.py:44
  87.9 5.8 %collective-permute-done.14 = f16[144,256]{1,0:T(8,128)(2,1)S(1)} collective-permute-done((f16[144,256]{1,0:T(8,128)(2,1)S(1)}, f16[144,256]{1,0:T(8,128)(2,1)S(1)}, u32[]{:S(2)}, u32[]{:S(2)}) %collective-permute-start.14) | collective-permute-done | bytes 73760 | tf_op jit(solution)/shard_map/ppermute | solution.py:44
  93.8 6.3 %collective-permute-done.27 = f16[144,512]{1,0:T(8,128)(2,1)S(1)} collective-permute-done((f16[144,512]{1,0:T(8,128)(2,1)S(1)}, f16[144,512]{1,0:T(8,128)(2,1)S(1)}, u32[]{:S(2)}, u32[]{:S(2)}) %collective-permute-start.27) | collective-permute-done | bytes 147488 | tf_op jit(solution)/shard_map/ppermute | solution.py:44
  100.1 6.1 %collective-permute-done.28 = f16[144,512]{1,0:T(8,128)(2,1)S(1)} collective-permute-done((f16[144,512]{1,0:T(8,128)(2,1)S(1)}, f16[144,512]{1,0:T(8,128)(2,1)S(1)}, u32[]{:S(2)}, u32[]{:S(2)}) %collective-permute-start.28) | collective-permute-done | bytes 147488 | tf_op jit(solution)/shard_map/ppermute | solution.py:44
  106.3 8.2 %collective-permute-done.29 = f16[144,512]{1,0:T(8,128)(2,1)S(1)} collective-permute-done((f16[144,512]{1,0:T(8,128)(2,1)S(1)}, f16[144,512]{1,0:T(8,128)(2,1)S(1)}, u32[]{:S(2)}, u32[]{:S(2)}) %collective-permute-start.29) | collective-permute-done | bytes 147488 | tf_op jit(solution)/shard_map/ppermute | solution.py:44
  114.9 2.3 %collective-permute-start.31 = (bf16[128,512]{1,0:T(8,128)(2,1)S(1)}, bf16[128,512]{1,0:T(8,128)(2,1)S(1)}, u32[]{:S(2)}, u32[]{:S(2)}) collective-permute-start(bf16[128,512]{1,0:T(8,128)(2,1)S(1)} %shard_map.90.refs_0_), channel_id=1, source_target_pairs={{0,32},{16,48},{32,0},{48,16},{1,33},{17,49},{33,1},{49,17},{2,34}... | collective-permute-start | bytes 393224 | tf_op jit(solution)/shard_map/ppermute | solution.py:44
  117.3 5.2 %collective-permute-done.30.refs_1_.refs_3_ = bf16[128,512]{1,0:T(8,128)(2,1)S(1)} collective-permute-done((bf16[128,512]{1,0:T(8,128)(2,1)S(1)}, bf16[128,512]{1,0:T(8,128)(2,1)S(1)}, u32[]{:S(2)}, u32[]{:S(2)}) %collective-permute-start.30) | collective-permute-done | bytes 131104 | tf_op jit(solution)/shard_map/ppermute | solution.py:44
  122.5 5.0 %collective-permute-done.32.refs_3_.refs_1_ = bf16[128,512]{1,0:T(8,128)(2,1)S(1)} collective-permute-done((bf16[128,512]{1,0:T(8,128)(2,1)S(1)}, bf16[128,512]{1,0:T(8,128)(2,1)S(1)}, u32[]{:S(2)}, u32[]{:S(2)}) %collective-permute-start.32) | collective-permute-done | bytes 131104 | tf_op jit(solution)/shard_map/ppermute | solution.py:44
  127.4 0.5 collective-permute-start.35
  128.0 0.7 collective-permute-done.34.refs_5_
  129.0 0.3 collective-permute-done.36.refs_7_
  129.3 2.1 %shard_map.91 = (f32[128,1024]{1,0:T(8,128)S(1)}, f32[144,1024]{1,0:T(8,128)S(1)}, f32[144,1024]{1,0:T(8,128)S(1)}, f32[144,1024]{1,0:T(8,128)S(1)}) custom-call(s32[3]{0:T(128)S(1)} %pad_add_fusion.flags.core_ref, bf16[128,512]{1,0:T(8,128)(2,1)S(1)} %shard_map.90.refs_0_, bf16[128,512]{1,0:T(8,128)(2,1)S(1)} %collective-permute-done.30.refs_1_.refs_3_, ...), custom_call_target="tpu_custom_call" | custom-call | flops 1073741824 | bytes 1048576 | tf_op jit(solution)/shard_map/pallas_call | solution.py:66
  131.5 1.3 collective-permute-start.49
  132.8 0.4 collective-permute-start.50
  133.2 0.5 collective-permute-start.51
  133.7 2.7 %collective-permute-done.49.refs_1_ = bf16[128,256]{1,0:T(8,128)(2,1)S(1)} collective-permute-done((bf16[128,256]{1,0:T(8,128)(2,1)S(1)}, bf16[128,256]{1,0:T(8,128)(2,1)S(1)}, u32[]{:S(2)}, u32[]{:S(2)}) %collective-permute-start.49) | collective-permute-done | bytes 65568 | tf_op jit(solution)/shard_map/ppermute | solution.py:44
  136.4 2.7 %collective-permute-done.50.refs_2_ = bf16[128,256]{1,0:T(8,128)(2,1)S(1)} collective-permute-done((bf16[128,256]{1,0:T(8,128)(2,1)S(1)}, bf16[128,256]{1,0:T(8,128)(2,1)S(1)}, u32[]{:S(2)}, u32[]{:S(2)}) %collective-permute-start.50) | collective-permute-done | bytes 65568 | tf_op jit(solution)/shard_map/ppermute | solution.py:44
  139.2 0.4 collective-permute-done.51.refs_3_
  139.5 1.3 shard_map.95
  140.8 0.5 collective-permute-start.52
  141.4 2.5 %collective-permute-start.53 = (bf16[128,1024]{1,0:T(8,128)(2,1)S(1)}, bf16[128,1024]{1,0:T(8,128)(2,1)S(1)}, u32[]{:S(2)}, u32[]{:S(2)}) collective-permute-start(bf16[128,1024]{1,0:T(8,128)(2,1)S(1)} %get-tuple-element.52), channel_id=1, source_target_pairs={{0,72},{1,73},{2,74},{3,75},{4,76},{5,77},{6,78},{7,79},{8,64},{9,... | collective-permute-start | bytes 786440 | tf_op jit(solution)/shard_map/ppermute | solution.py:40
  143.8 1.4 collective-permute-start.54
  145.3 1.8 shard_map.94
  147.2 1.8 collective-permute-start.41
  149.1 7.7 %collective-permute-done.43 = f16[144,1024]{1,0:T(8,128)(2,1)S(1)} collective-permute-done((f16[144,1024]{1,0:T(8,128)(2,1)S(1)}, f16[144,1024]{1,0:T(8,128)(2,1)S(1)}, u32[]{:S(2)}, u32[]{:S(2)}) %collective-permute-start.43) | collective-permute-done | bytes 294944 | tf_op jit(solution)/shard_map/ppermute | solution.py:44
  156.8 0.2 collective-permute-start.46
  157.1 4.0 %collective-permute-done.41 = f16[144,1024]{1,0:T(8,128)(2,1)S(1)} collective-permute-done((f16[144,1024]{1,0:T(8,128)(2,1)S(1)}, f16[144,1024]{1,0:T(8,128)(2,1)S(1)}, u32[]{:S(2)}, u32[]{:S(2)}) %collective-permute-start.41) | collective-permute-done | bytes 294944 | tf_op jit(solution)/shard_map/ppermute | solution.py:44
  161.1 2.3 %collective-permute-start.47 = (bf16[1024,256]{1,0:T(8,128)(2,1)S(1)}, bf16[1024,256]{1,0:T(8,128)(2,1)S(1)}, u32[]{:S(2)}, u32[]{:S(2)}) collective-permute-start(bf16[1024,256]{1,0:T(8,128)(2,1)S(1)} %get-tuple-element.47), channel_id=1, source_target_pairs={{0,72},{1,73},{2,74},{3,75},{4,76},{5,77},{6,78},{7,79},{8,64},{9,... | collective-permute-start | bytes 1572872 | tf_op jit(solution)/shard_map/ppermute | solution.py:40
  163.6 0.2 fusion.1.in_ref
  163.8 0.9 convert_add_fusion
  164.8 0.6 shard_map.92
  165.3 0.7 collective-permute-start.44
  166.0 1.8 collective-permute-start.45
  167.8 0.3 collective-permute-done.46
  168.1 19.2 %collective-permute-done.47 = bf16[1024,256]{1,0:T(8,128)(2,1)S(1)} collective-permute-done((bf16[1024,256]{1,0:T(8,128)(2,1)S(1)}, bf16[1024,256]{1,0:T(8,128)(2,1)S(1)}, u32[]{:S(2)}, u32[]{:S(2)}) %collective-permute-start.47) | collective-permute-done | bytes 524320 | tf_op jit(solution)/shard_map/ppermute | solution.py:40
  187.2 1.2 convert_add_fusion.1
  188.4 1.3 shard_map.93
  (101 shorter events, 2.5 us)
Async XLA Ops:
  0.6 3.8 %copy-start.2 = (bf16[128,1024]{1,0:T(8,128)(2,1)S(1)}, bf16[128,1024]{1,0:T(8,128)(2,1)}, u32[]{:S(2)}) copy-start(bf16[128,1024]{1,0:T(8,128)(2,1)} %refs_8_.1) | copy-start | bytes 786436
  0.6 7.4 %copy-start.3 = (bf16[256,512]{1,0:T(8,128)(2,1)S(1)}, bf16[256,512]{1,0:T(8,128)(2,1)}, u32[]{:S(2)}) copy-start(bf16[256,512]{1,0:T(8,128)(2,1)} %param.6) | copy-start | bytes 786436
  1.7 6.4 %collective-permute-start.15 = (bf16[128,512]{1,0:T(8,128)(2,1)S(1)}, bf16[128,512]{1,0:T(8,128)(2,1)S(1)}, u32[]{:S(2)}, u32[]{:S(2)}) collective-permute-start(bf16[128,512]{1,0:T(8,128)(2,1)S(1)} %get-tuple-element.57), channel_id=1, source_target_pairs={{0,0},{1,1},{2,18},{3,19},{4,36},{5,37},{6,54},{7,55},{8,8},{9,9},... | collective-permute-start | bytes 393224 | tf_op jit(solution)/shard_map/ppermute | solution.py:40
  2.4 6.4 %collective-permute-start.16 = (bf16[128,512]{1,0:T(8,128)(2,1)S(1)}, bf16[128,512]{1,0:T(8,128)(2,1)S(1)}, u32[]{:S(2)}, u32[]{:S(2)}) collective-permute-start(bf16[128,512]{1,0:T(8,128)(2,1)S(1)} %get-tuple-element.56), channel_id=1, source_target_pairs={{0,8},{1,9},{2,26},{3,27},{4,44},{5,45},{6,62},{7,63},{8,0},{9,1},... | collective-permute-start | bytes 393224 | tf_op jit(solution)/shard_map/ppermute | solution.py:40
  4.5 27.6 %collective-permute-start.10 = (bf16[128,1024]{1,0:T(8,128)(2,1)S(1)}, bf16[128,1024]{1,0:T(8,128)(2,1)S(1)}, u32[]{:S(2)}, u32[]{:S(2)}) collective-permute-start(bf16[128,1024]{1,0:T(8,128)(2,1)S(1)} %copy-done.2), channel_id=1, source_target_pairs={{0,64},{1,65},{2,66},{3,67},{4,68},{5,69},{6,70},{7,71},{8,72},{9,... | collective-permute-start | bytes 786440 | tf_op jit(solution)/shard_map/ppermute | solution.py:40
  8.1 24.1 %collective-permute-start.11 = (bf16[128,1024]{1,0:T(8,128)(2,1)S(1)}, bf16[128,1024]{1,0:T(8,128)(2,1)S(1)}, u32[]{:S(2)}, u32[]{:S(2)}) collective-permute-start(bf16[128,1024]{1,0:T(8,128)(2,1)S(1)} %copy-done.2), channel_id=1, source_target_pairs={{0,72},{1,73},{2,74},{3,75},{4,76},{5,77},{6,78},{7,79},{8,64},{9,... | collective-permute-start | bytes 786440 | tf_op jit(solution)/shard_map/ppermute | solution.py:40
  8.1 24.3 %collective-permute-start.9 = (bf16[128,1024]{1,0:T(8,128)(2,1)S(1)}, bf16[128,1024]{1,0:T(8,128)(2,1)S(1)}, u32[]{:S(2)}, u32[]{:S(2)}) collective-permute-start(bf16[128,1024]{1,0:T(8,128)(2,1)S(1)} %copy-done.2), channel_id=1, source_target_pairs={{0,8},{1,9},{2,10},{3,11},{4,12},{5,13},{6,14},{7,15},{8,0},{9,1},... | collective-permute-start | bytes 786440 | tf_op jit(solution)/shard_map/ppermute | solution.py:40
  8.1 3.4 %collective-permute-start = (bf16[128,512]{1,0:T(8,128)(2,1)S(1)}, bf16[128,512]{1,0:T(8,128)(2,1)S(1)}, u32[]{:S(2)}, u32[]{:S(2)}) collective-permute-start(bf16[128,512]{1,0:T(8,128)(2,1)S(1)} %get-tuple-element.59), channel_id=1, source_target_pairs={{0,0},{1,1},{2,18},{3,19},{4,36},{5,37},{6,54},{7,55},{8,8},{9,9},... | collective-permute-start | bytes 393224 | tf_op jit(solution)/shard_map/ppermute | solution.py:40
  8.8 13.4 %collective-permute-start.1 = (bf16[128,512]{1,0:T(8,128)(2,1)S(1)}, bf16[128,512]{1,0:T(8,128)(2,1)S(1)}, u32[]{:S(2)}, u32[]{:S(2)}) collective-permute-start(bf16[128,512]{1,0:T(8,128)(2,1)S(1)} %get-tuple-element.58), channel_id=1, source_target_pairs={{0,8},{1,9},{2,26},{3,27},{4,44},{5,45},{6,62},{7,63},{8,0},{9,1},... | collective-permute-start | bytes 393224 | tf_op jit(solution)/shard_map/ppermute | solution.py:40
  11.0 21.3 %copy-start = (bf16[1024,128]{1,0:T(8,128)(2,1)S(1)}, bf16[1024,128]{1,0:T(8,128)(2,1)}, u32[]{:S(2)}) copy-start(bf16[1024,128]{1,0:T(8,128)(2,1)} %a_ref.1) | copy-start | bytes 786436
  11.0 21.3 %copy-start.1 = (bf16[1024,128]{1,0:T(8,128)(2,1)S(1)}, bf16[1024,128]{1,0:T(8,128)(2,1)}, u32[]{:S(2)}) copy-start(bf16[1024,128]{1,0:T(8,128)(2,1)} %b_ref.1) | copy-start | bytes 786436
  11.6 22.8 %collective-permute-start.17 = (bf16[128,1024]{1,0:T(8,128)(2,1)S(1)}, bf16[128,1024]{1,0:T(8,128)(2,1)S(1)}, u32[]{:S(2)}, u32[]{:S(2)}) collective-permute-start(bf16[128,1024]{1,0:T(8,128)(2,1)S(1)} %shard_map.86.refs_0_.refs_4_), channel_id=1, source_target_pairs={{0,2},{2,4},{4,6},{6,0},{1,3},{3,5},{5,7},{7,1},{8,10},{10,12},{12... | collective-permute-start | bytes 786440 | tf_op jit(solution)/shard_map/ppermute | solution.py:44
  22.2 14.5 %collective-permute-start.18 = (bf16[128,1024]{1,0:T(8,128)(2,1)S(1)}, bf16[128,1024]{1,0:T(8,128)(2,1)S(1)}, u32[]{:S(2)}, u32[]{:S(2)}) collective-permute-start(bf16[128,1024]{1,0:T(8,128)(2,1)S(1)} %shard_map.86.refs_0_.refs_4_), channel_id=1, source_target_pairs={{0,4},{2,6},{4,0},{6,2},{1,5},{3,7},{5,1},{7,3},{8,12},{10,14},{12... | collective-permute-start | bytes 786440 | tf_op jit(solution)/shard_map/ppermute | solution.py:44
  32.1 7.9 %collective-permute-start.19 = (bf16[128,1024]{1,0:T(8,128)(2,1)S(1)}, bf16[128,1024]{1,0:T(8,128)(2,1)S(1)}, u32[]{:S(2)}, u32[]{:S(2)}) collective-permute-start(bf16[128,1024]{1,0:T(8,128)(2,1)S(1)} %shard_map.86.refs_0_.refs_4_), channel_id=1, source_target_pairs={{0,6},{2,0},{4,2},{6,4},{1,7},{3,1},{5,3},{7,5},{8,14},{10,8},{12,... | collective-permute-start | bytes 786440 | tf_op jit(solution)/shard_map/ppermute | solution.py:44
  32.1 8.9 %collective-permute-start.20 = (bf16[128,1024]{1,0:T(8,128)(2,1)S(1)}, bf16[128,1024]{1,0:T(8,128)(2,1)S(1)}, u32[]{:S(2)}, u32[]{:S(2)}) collective-permute-start(bf16[128,1024]{1,0:T(8,128)(2,1)S(1)} %shard_map.86.refs_0_.refs_4_), channel_id=1, source_target_pairs={{0,1},{1,0},{2,3},{3,2},{4,5},{5,4},{6,7},{7,6},{8,9},{9,8},{10,11... | collective-permute-start | bytes 786440 | tf_op jit(solution)/shard_map/ppermute | solution.py:48
  32.3 22.3 %collective-permute-start.24 = (bf16[1024,256]{1,0:T(8,128)(2,1)S(1)}, bf16[1024,256]{1,0:T(8,128)(2,1)S(1)}, u32[]{:S(2)}, u32[]{:S(2)}) collective-permute-start(bf16[1024,256]{1,0:T(8,128)(2,1)S(1)} %shard_map.87.refs_8_), channel_id=1, source_target_pairs={{0,8},{1,9},{2,10},{3,11},{4,12},{5,13},{6,14},{7,15},{8,0},{9,1},... | collective-permute-start | bytes 1572872 | tf_op jit(solution)/shard_map/ppermute | solution.py:40
  34.4 15.3 %collective-permute-start.2 = (bf16[128,1024]{1,0:T(8,128)(2,1)S(1)}, bf16[128,1024]{1,0:T(8,128)(2,1)S(1)}, u32[]{:S(2)}, u32[]{:S(2)}) collective-permute-start(bf16[128,1024]{1,0:T(8,128)(2,1)S(1)} %shard_map.84.refs_0_.refs_4_), channel_id=1, source_target_pairs={{0,2},{2,4},{4,6},{6,0},{1,3},{3,5},{5,7},{7,1},{8,10},{10,12},{12... | collective-permute-start | bytes 786440 | tf_op jit(solution)/shard_map/ppermute | solution.py:44
  36.7 17.4 %collective-permute-start.3 = (bf16[128,1024]{1,0:T(8,128)(2,1)S(1)}, bf16[128,1024]{1,0:T(8,128)(2,1)S(1)}, u32[]{:S(2)}, u32[]{:S(2)}) collective-permute-start(bf16[128,1024]{1,0:T(8,128)(2,1)S(1)} %shard_map.84.refs_0_.refs_4_), channel_id=1, source_target_pairs={{0,4},{2,6},{4,0},{6,2},{1,5},{3,7},{5,1},{7,3},{8,12},{10,14},{12... | collective-permute-start | bytes 786440 | tf_op jit(solution)/shard_map/ppermute | solution.py:44
  40.0 14.0 %collective-permute-start.4 = (bf16[128,1024]{1,0:T(8,128)(2,1)S(1)}, bf16[128,1024]{1,0:T(8,128)(2,1)S(1)}, u32[]{:S(2)}, u32[]{:S(2)}) collective-permute-start(bf16[128,1024]{1,0:T(8,128)(2,1)S(1)} %shard_map.84.refs_0_.refs_4_), channel_id=1, source_target_pairs={{0,6},{2,0},{4,2},{6,4},{1,7},{3,1},{5,3},{7,5},{8,14},{10,8},{12,... | collective-permute-start | bytes 786440 | tf_op jit(solution)/shard_map/ppermute | solution.py:44
  41.0 13.2 %collective-permute-start.5 = (bf16[128,1024]{1,0:T(8,128)(2,1)S(1)}, bf16[128,1024]{1,0:T(8,128)(2,1)S(1)}, u32[]{:S(2)}, u32[]{:S(2)}) collective-permute-start(bf16[128,1024]{1,0:T(8,128)(2,1)S(1)} %shard_map.84.refs_0_.refs_4_), channel_id=1, source_target_pairs={{0,1},{1,0},{2,3},{3,2},{4,5},{5,4},{6,7},{7,6},{8,9},{9,8},{10,11... | collective-permute-start | bytes 786440 | tf_op jit(solution)/shard_map/ppermute | solution.py:48
  49.7 16.3 %collective-permute-start.25 = (bf16[1024,256]{1,0:T(8,128)(2,1)S(1)}, bf16[1024,256]{1,0:T(8,128)(2,1)S(1)}, u32[]{:S(2)}, u32[]{:S(2)}) collective-permute-start(bf16[1024,256]{1,0:T(8,128)(2,1)S(1)} %shard_map.87.refs_8_), channel_id=1, source_target_pairs={{0,64},{1,65},{2,66},{3,67},{4,68},{5,69},{6,70},{7,71},{8,72},{9,... | collective-permute-start | bytes 1572872 | tf_op jit(solution)/shard_map/ppermute | solution.py:40
  54.1 23.0 %collective-permute-start.26 = (bf16[1024,256]{1,0:T(8,128)(2,1)S(1)}, bf16[1024,256]{1,0:T(8,128)(2,1)S(1)}, u32[]{:S(2)}, u32[]{:S(2)}) collective-permute-start(bf16[1024,256]{1,0:T(8,128)(2,1)S(1)} %shard_map.87.refs_8_), channel_id=1, source_target_pairs={{0,72},{1,73},{2,74},{3,75},{4,76},{5,77},{6,78},{7,79},{8,64},{9,... | collective-permute-start | bytes 1572872 | tf_op jit(solution)/shard_map/ppermute | solution.py:40
  54.1 1.6 collective-permute-start.6
  54.2 1.9 collective-permute-start.7
  54.7 1.8 collective-permute-start.8
  55.7 21.4 %collective-permute-start.21 = (bf16[128,1024]{1,0:T(8,128)(2,1)S(1)}, bf16[128,1024]{1,0:T(8,128)(2,1)S(1)}, u32[]{:S(2)}, u32[]{:S(2)}) collective-permute-start(bf16[128,1024]{1,0:T(8,128)(2,1)S(1)} %collective-permute-done.17.refs_1_.refs_5_), channel_id=1, source_target_pairs={{0,1},{1,0},{2,3},{3,2},{4,5},{5,4},{6,7},{7,6},{8,9},{9,8},{10,11... | collective-permute-start | bytes 786440 | tf_op jit(solution)/shard_map/ppermute | solution.py:48
  56.1 21.6 %collective-permute-start.22 = (bf16[128,1024]{1,0:T(8,128)(2,1)S(1)}, bf16[128,1024]{1,0:T(8,128)(2,1)S(1)}, u32[]{:S(2)}, u32[]{:S(2)}) collective-permute-start(bf16[128,1024]{1,0:T(8,128)(2,1)S(1)} %collective-permute-done.18.refs_2_.refs_6_), channel_id=1, source_target_pairs={{0,1},{1,0},{2,3},{3,2},{4,5},{5,4},{6,7},{7,6},{8,9},{9,8},{10,11... | collective-permute-start | bytes 786440 | tf_op jit(solution)/shard_map/ppermute | solution.py:48
  56.4 21.3 %collective-permute-start.23 = (bf16[128,1024]{1,0:T(8,128)(2,1)S(1)}, bf16[128,1024]{1,0:T(8,128)(2,1)S(1)}, u32[]{:S(2)}, u32[]{:S(2)}) collective-permute-start(bf16[128,1024]{1,0:T(8,128)(2,1)S(1)} %collective-permute-done.19.refs_3_.refs_7_), channel_id=1, source_target_pairs={{0,1},{1,0},{2,3},{3,2},{4,5},{5,4},{6,7},{7,6},{8,9},{9,8},{10,11... | collective-permute-start | bytes 786440 | tf_op jit(solution)/shard_map/ppermute | solution.py:48
  66.0 48.9 %collective-permute-start.37 = (bf16[1024,256]{1,0:T(8,128)(2,1)S(1)}, bf16[1024,256]{1,0:T(8,128)(2,1)S(1)}, u32[]{:S(2)}, u32[]{:S(2)}) collective-permute-start(bf16[1024,256]{1,0:T(8,128)(2,1)S(1)} %shard_map.87.refs_8_), channel_id=1, source_target_pairs={{0,1},{1,0},{2,3},{3,2},{4,5},{5,4},{6,7},{7,6},{8,9},{9,8},{10,11... | collective-permute-start | bytes 1572872 | tf_op jit(solution)/shard_map/ppermute | solution.py:48
  77.1 50.8 %collective-permute-start.38 = (bf16[1024,256]{1,0:T(8,128)(2,1)S(1)}, bf16[1024,256]{1,0:T(8,128)(2,1)S(1)}, u32[]{:S(2)}, u32[]{:S(2)}) collective-permute-start(bf16[1024,256]{1,0:T(8,128)(2,1)S(1)} %collective-permute-done.24.refs_9_), channel_id=1, source_target_pairs={{0,1},{1,0},{2,3},{3,2},{4,5},{5,4},{6,7},{7,6},{8,9},{9,8},{10,11... | collective-permute-start | bytes 1572872 | tf_op jit(solution)/shard_map/ppermute | solution.py:48
  77.1 50.9 %collective-permute-start.39 = (bf16[1024,256]{1,0:T(8,128)(2,1)S(1)}, bf16[1024,256]{1,0:T(8,128)(2,1)S(1)}, u32[]{:S(2)}, u32[]{:S(2)}) collective-permute-start(bf16[1024,256]{1,0:T(8,128)(2,1)S(1)} %collective-permute-done.25.refs_10_), channel_id=1, source_target_pairs={{0,1},{1,0},{2,3},{3,2},{4,5},{5,4},{6,7},{7,6},{8,9},{9,8},{10,11... | collective-permute-start | bytes 1572872 | tf_op jit(solution)/shard_map/ppermute | solution.py:48
  77.6 50.4 %collective-permute-start.40 = (bf16[1024,256]{1,0:T(8,128)(2,1)S(1)}, bf16[1024,256]{1,0:T(8,128)(2,1)S(1)}, u32[]{:S(2)}, u32[]{:S(2)}) collective-permute-start(bf16[1024,256]{1,0:T(8,128)(2,1)S(1)} %collective-permute-done.26.refs_11_), channel_id=1, source_target_pairs={{0,1},{1,0},{2,3},{3,2},{4,5},{5,4},{6,7},{7,6},{8,9},{9,8},{10,11... | collective-permute-start | bytes 1572872 | tf_op jit(solution)/shard_map/ppermute | solution.py:48
  77.7 5.8 %collective-permute-start.12 = (f16[144,256]{1,0:T(8,128)(2,1)S(1)}, f16[144,256]{1,0:T(8,128)(2,1)S(1)}, u32[]{:S(2)}, u32[]{:S(2)}) collective-permute-start(f16[144,256]{1,0:T(8,128)(2,1)S(1)} %convert_element_type.84), channel_id=1, source_target_pairs={{0,16},{16,32},{32,48},{48,0},{1,17},{17,33},{33,49},{49,1},{2,18}... | collective-permute-start | bytes 221192 | tf_op jit(solution)/shard_map/ppermute | solution.py:44
  83.5 4.4 %collective-permute-start.13 = (f16[144,256]{1,0:T(8,128)(2,1)S(1)}, f16[144,256]{1,0:T(8,128)(2,1)S(1)}, u32[]{:S(2)}, u32[]{:S(2)}) collective-permute-start(f16[144,256]{1,0:T(8,128)(2,1)S(1)} %convert_element_type.86), channel_id=1, source_target_pairs={{0,48},{16,0},{32,16},{48,32},{1,49},{17,1},{33,17},{49,33},{2,50}... | collective-permute-start | bytes 221192 | tf_op jit(solution)/shard_map/ppermute | solution.py:44
  87.9 5.9 %collective-permute-start.14 = (f16[144,256]{1,0:T(8,128)(2,1)S(1)}, f16[144,256]{1,0:T(8,128)(2,1)S(1)}, u32[]{:S(2)}, u32[]{:S(2)}) collective-permute-start(f16[144,256]{1,0:T(8,128)(2,1)S(1)} %convert_element_type.88), channel_id=1, source_target_pairs={{0,32},{16,48},{32,0},{48,16},{1,33},{17,49},{33,1},{49,17},{2,34}... | collective-permute-start | bytes 221192 | tf_op jit(solution)/shard_map/ppermute | solution.py:44
  93.7 6.4 %collective-permute-start.27 = (f16[144,512]{1,0:T(8,128)(2,1)S(1)}, f16[144,512]{1,0:T(8,128)(2,1)S(1)}, u32[]{:S(2)}, u32[]{:S(2)}) collective-permute-start(f16[144,512]{1,0:T(8,128)(2,1)S(1)} %convert_element_type.90), channel_id=1, source_target_pairs={{0,16},{16,32},{32,48},{48,0},{1,17},{17,33},{33,49},{49,1},{2,18}... | collective-permute-start | bytes 442376 | tf_op jit(solution)/shard_map/ppermute | solution.py:44
  100.1 6.2 %collective-permute-start.28 = (f16[144,512]{1,0:T(8,128)(2,1)S(1)}, f16[144,512]{1,0:T(8,128)(2,1)S(1)}, u32[]{:S(2)}, u32[]{:S(2)}) collective-permute-start(f16[144,512]{1,0:T(8,128)(2,1)S(1)} %convert_element_type.92), channel_id=1, source_target_pairs={{0,48},{16,0},{32,16},{48,32},{1,49},{17,1},{33,17},{49,33},{2,50}... | collective-permute-start | bytes 442376 | tf_op jit(solution)/shard_map/ppermute | solution.py:44
  106.3 8.2 %collective-permute-start.29 = (f16[144,512]{1,0:T(8,128)(2,1)S(1)}, f16[144,512]{1,0:T(8,128)(2,1)S(1)}, u32[]{:S(2)}, u32[]{:S(2)}) collective-permute-start(f16[144,512]{1,0:T(8,128)(2,1)S(1)} %convert_element_type.94), channel_id=1, source_target_pairs={{0,32},{16,48},{32,0},{48,16},{1,33},{17,49},{33,1},{49,17},{2,34}... | collective-permute-start | bytes 442376 | tf_op jit(solution)/shard_map/ppermute | solution.py:44
  114.8 7.7 %collective-permute-start.30 = (bf16[128,512]{1,0:T(8,128)(2,1)S(1)}, bf16[128,512]{1,0:T(8,128)(2,1)S(1)}, u32[]{:S(2)}, u32[]{:S(2)}) collective-permute-start(bf16[128,512]{1,0:T(8,128)(2,1)S(1)} %shard_map.90.refs_0_), channel_id=1, source_target_pairs={{0,16},{16,32},{32,48},{48,0},{1,17},{17,33},{33,49},{49,1},{2,18}... | collective-permute-start | bytes 393224 | tf_op jit(solution)/shard_map/ppermute | solution.py:44
  114.9 7.6 %collective-permute-start.31 = (bf16[128,512]{1,0:T(8,128)(2,1)S(1)}, bf16[128,512]{1,0:T(8,128)(2,1)S(1)}, u32[]{:S(2)}, u32[]{:S(2)}) collective-permute-start(bf16[128,512]{1,0:T(8,128)(2,1)S(1)} %shard_map.90.refs_0_), channel_id=1, source_target_pairs={{0,32},{16,48},{32,0},{48,16},{1,33},{17,49},{33,1},{49,17},{2,34}... | collective-permute-start | bytes 393224 | tf_op jit(solution)/shard_map/ppermute | solution.py:44
  122.5 5.0 %collective-permute-start.32 = (bf16[128,512]{1,0:T(8,128)(2,1)S(1)}, bf16[128,512]{1,0:T(8,128)(2,1)S(1)}, u32[]{:S(2)}, u32[]{:S(2)}) collective-permute-start(bf16[128,512]{1,0:T(8,128)(2,1)S(1)} %shard_map.90.refs_0_), channel_id=1, source_target_pairs={{0,48},{16,0},{32,16},{48,32},{1,49},{17,1},{33,17},{49,33},{2,50}... | collective-permute-start | bytes 393224 | tf_op jit(solution)/shard_map/ppermute | solution.py:44
  122.5 5.0 %collective-permute-start.33 = (bf16[128,512]{1,0:T(8,128)(2,1)S(1)}, bf16[128,512]{1,0:T(8,128)(2,1)S(1)}, u32[]{:S(2)}, u32[]{:S(2)}) collective-permute-start(bf16[128,512]{1,0:T(8,128)(2,1)S(1)} %shard_map.90.refs_0_), channel_id=1, source_target_pairs={{0,1},{1,0},{2,3},{3,2},{4,5},{5,4},{6,7},{7,6},{8,9},{9,8},{10,11... | collective-permute-start | bytes 393224 | tf_op jit(solution)/shard_map/ppermute | solution.py:48
  127.4 1.3 collective-permute-start.34
  127.4 1.5 collective-permute-start.35
  128.0 1.3 collective-permute-start.36
  131.4 15.8 %collective-permute-start.42 = (f16[144,1024]{1,0:T(8,128)(2,1)S(1)}, f16[144,1024]{1,0:T(8,128)(2,1)S(1)}, u32[]{:S(2)}, u32[]{:S(2)}) collective-permute-start(f16[144,1024]{1,0:T(8,128)(2,1)S(1)} %convert_element_type.98), channel_id=1, source_target_pairs={{0,6},{2,0},{4,2},{6,4},{1,7},{3,1},{5,3},{7,5},{8,14},{10,8},{12,... | collective-permute-start | bytes 884744 | tf_op jit(solution)/shard_map/ppermute | solution.py:44
  131.5 4.9 %collective-permute-start.49 = (bf16[128,256]{1,0:T(8,128)(2,1)S(1)}, bf16[128,256]{1,0:T(8,128)(2,1)S(1)}, u32[]{:S(2)}, u32[]{:S(2)}) collective-permute-start(bf16[128,256]{1,0:T(8,128)(2,1)S(1)} %get-tuple-element.49.refs_0_), channel_id=1, source_target_pairs={{0,48},{16,0},{32,16},{48,32},{1,49},{17,1},{33,17},{49,33},{2,50}... | collective-permute-start | bytes 196616 | tf_op jit(solution)/shard_map/ppermute | solution.py:44
  132.8 6.4 %collective-permute-start.50 = (bf16[128,256]{1,0:T(8,128)(2,1)S(1)}, bf16[128,256]{1,0:T(8,128)(2,1)S(1)}, u32[]{:S(2)}, u32[]{:S(2)}) collective-permute-start(bf16[128,256]{1,0:T(8,128)(2,1)S(1)} %get-tuple-element.49.refs_0_), channel_id=1, source_target_pairs={{0,32},{16,48},{32,0},{48,16},{1,33},{17,49},{33,1},{49,17},{2,34}... | collective-permute-start | bytes 196616 | tf_op jit(solution)/shard_map/ppermute | solution.py:44
  133.2 6.3 %collective-permute-start.51 = (bf16[128,256]{1,0:T(8,128)(2,1)S(1)}, bf16[128,256]{1,0:T(8,128)(2,1)S(1)}, u32[]{:S(2)}, u32[]{:S(2)}) collective-permute-start(bf16[128,256]{1,0:T(8,128)(2,1)S(1)} %get-tuple-element.49.refs_0_), channel_id=1, source_target_pairs={{0,16},{16,32},{32,48},{48,0},{1,17},{17,33},{33,49},{49,1},{2,18}... | collective-permute-start | bytes 196616 | tf_op jit(solution)/shard_map/ppermute | solution.py:44
  140.8 22.7 %collective-permute-start.52 = (bf16[128,1024]{1,0:T(8,128)(2,1)S(1)}, bf16[128,1024]{1,0:T(8,128)(2,1)S(1)}, u32[]{:S(2)}, u32[]{:S(2)}) collective-permute-start(bf16[128,1024]{1,0:T(8,128)(2,1)S(1)} %get-tuple-element.51), channel_id=1, source_target_pairs={{0,8},{1,9},{2,10},{3,11},{4,12},{5,13},{6,14},{7,15},{8,0},{9,1},... | collective-permute-start | bytes 786440 | tf_op jit(solution)/shard_map/ppermute | solution.py:40
  141.4 22.5 %collective-permute-start.53 = (bf16[128,1024]{1,0:T(8,128)(2,1)S(1)}, bf16[128,1024]{1,0:T(8,128)(2,1)S(1)}, u32[]{:S(2)}, u32[]{:S(2)}) collective-permute-start(bf16[128,1024]{1,0:T(8,128)(2,1)S(1)} %get-tuple-element.52), channel_id=1, source_target_pairs={{0,72},{1,73},{2,74},{3,75},{4,76},{5,77},{6,78},{7,79},{8,64},{9,... | collective-permute-start | bytes 786440 | tf_op jit(solution)/shard_map/ppermute | solution.py:40
  143.8 20.0 %collective-permute-start.54 = (bf16[128,1024]{1,0:T(8,128)(2,1)S(1)}, bf16[128,1024]{1,0:T(8,128)(2,1)S(1)}, u32[]{:S(2)}, u32[]{:S(2)}) collective-permute-start(bf16[128,1024]{1,0:T(8,128)(2,1)S(1)} %get-tuple-element.53), channel_id=1, source_target_pairs={{0,64},{1,65},{2,66},{3,67},{4,68},{5,69},{6,70},{7,71},{8,72},{9,... | collective-permute-start | bytes 786440 | tf_op jit(solution)/shard_map/ppermute | solution.py:40
  145.3 11.5 %collective-permute-start.43 = (f16[144,1024]{1,0:T(8,128)(2,1)S(1)}, f16[144,1024]{1,0:T(8,128)(2,1)S(1)}, u32[]{:S(2)}, u32[]{:S(2)}) collective-permute-start(f16[144,1024]{1,0:T(8,128)(2,1)S(1)} %convert_element_type.100), channel_id=1, source_target_pairs={{0,4},{2,6},{4,0},{6,2},{1,5},{3,7},{5,1},{7,3},{8,12},{10,14},{12... | collective-permute-start | bytes 884744 | tf_op jit(solution)/shard_map/ppermute | solution.py:44
  147.2 13.8 %collective-permute-start.41 = (f16[144,1024]{1,0:T(8,128)(2,1)S(1)}, f16[144,1024]{1,0:T(8,128)(2,1)S(1)}, u32[]{:S(2)}, u32[]{:S(2)}) collective-permute-start(f16[144,1024]{1,0:T(8,128)(2,1)S(1)} %convert_element_type.96), channel_id=1, source_target_pairs={{0,2},{2,4},{4,6},{6,0},{1,3},{3,5},{5,7},{7,1},{8,10},{10,12},{12... | collective-permute-start | bytes 884744 | tf_op jit(solution)/shard_map/ppermute | solution.py:44
  156.8 11.3 %collective-permute-start.46 = (bf16[1024,256]{1,0:T(8,128)(2,1)S(1)}, bf16[1024,256]{1,0:T(8,128)(2,1)S(1)}, u32[]{:S(2)}, u32[]{:S(2)}) collective-permute-start(bf16[1024,256]{1,0:T(8,128)(2,1)S(1)} %get-tuple-element.46), channel_id=1, source_target_pairs={{0,8},{1,9},{2,10},{3,11},{4,12},{5,13},{6,14},{7,15},{8,0},{9,1},... | collective-permute-start | bytes 1572872 | tf_op jit(solution)/shard_map/ppermute | solution.py:40
  161.1 26.2 %collective-permute-start.47 = (bf16[1024,256]{1,0:T(8,128)(2,1)S(1)}, bf16[1024,256]{1,0:T(8,128)(2,1)S(1)}, u32[]{:S(2)}, u32[]{:S(2)}) collective-permute-start(bf16[1024,256]{1,0:T(8,128)(2,1)S(1)} %get-tuple-element.47), channel_id=1, source_target_pairs={{0,72},{1,73},{2,74},{3,75},{4,76},{5,77},{6,78},{7,79},{8,64},{9,... | collective-permute-start | bytes 1572872 | tf_op jit(solution)/shard_map/ppermute | solution.py:40
  163.5 23.7 %collective-permute-start.48 = (bf16[1024,256]{1,0:T(8,128)(2,1)S(1)}, bf16[1024,256]{1,0:T(8,128)(2,1)S(1)}, u32[]{:S(2)}, u32[]{:S(2)}) collective-permute-start(bf16[1024,256]{1,0:T(8,128)(2,1)S(1)} %get-tuple-element.48), channel_id=1, source_target_pairs={{0,64},{1,65},{2,66},{3,67},{4,68},{5,69},{6,70},{7,71},{8,72},{9,... | collective-permute-start | bytes 1572872 | tf_op jit(solution)/shard_map/ppermute | solution.py:40
  165.3 23.1 %collective-permute-start.44 = (bf16[128,512]{1,0:T(8,128)(2,1)S(1)}, bf16[128,512]{1,0:T(8,128)(2,1)S(1)}, u32[]{:S(2)}, u32[]{:S(2)}) collective-permute-start(bf16[128,512]{1,0:T(8,128)(2,1)S(1)} %get-tuple-element.43), channel_id=1, source_target_pairs={{0,0},{1,1},{18,2},{19,3},{36,4},{37,5},{54,6},{55,7},{8,8},{9,9},... | collective-permute-start | bytes 393224 | tf_op jit(solution)/shard_map/ppermute | solution.py:40
  166.0 22.4 %collective-permute-start.45 = (bf16[128,512]{1,0:T(8,128)(2,1)S(1)}, bf16[128,512]{1,0:T(8,128)(2,1)S(1)}, u32[]{:S(2)}, u32[]{:S(2)}) collective-permute-start(bf16[128,512]{1,0:T(8,128)(2,1)S(1)} %get-tuple-element.44), channel_id=1, source_target_pairs={{8,0},{9,1},{26,2},{27,3},{44,4},{45,5},{62,6},{63,7},{0,8},{1,9},... | collective-permute-start | bytes 393224 | tf_op jit(solution)/shard_map/ppermute | solution.py:40
